TPU v7x, 256 devices: a whole 4x4x8 slice. The times are simulated.
256 devices in a mesh: lb: 8 (over z), rb: 16 (over x, y), wa: 2 (over core).
Axes of the slice: x: 4, y: 4, z: 8, core: 2. Of those that a mesh axis runs over, the one named last changes fastest.
Arguments:
- initial_guess: bfloat16 [8192, 4, 128], P(('lb', 'rb')), may hold values from -6 to 6
- left_environment: bfloat16 [8, 8, 16, 64, 8192], P('wa', None, 'rb', None, 'lb'), may hold values from -12 to 12, as said below
- right_environment: bfloat16 [128, 8, 128], replicated, may hold values from -12 to 12, as said below
- operator_blocks: float32 [16, 4, 4], replicated, may hold values from -4 to 4
- operator_pairs: int32 [16, 2], replicated, may hold values from 0 to 7
Outputs:
- ritz_vector: float32 [8192, 4, 128], P(('lb', 'rb'))
- residual: float32 [8192, 4, 128], P(('lb', 'rb'))
Inputs may be any that keep to these rules, and one draw needn't show every extreme that they name: `operator_pairs`: each row names the left and the right MPO index of one operator block; blocks with the same pair add. `left_environment`: for each MPO index the [8192, 8192] matrix is symmetric. `right_environment`: for each MPO index the matrix over the two right bond states is symmetric.
All inputs are finite; a program needn't handle non-finite values.
Results may differ from a plain program's by a relative error of at most 0.014.
Values may be sent and summed in bfloat16 or wider, within the bound.
A program may use at most 128 MiB of HBM per device.

v0:
```python
import functools

import jax
import jax.numpy as jnp
from jax import lax
from jax.sharding import Mesh
from jax.sharding import PartitionSpec as P

ITERS = 3
SWEEPS = 8
RB = ("rb_0", "rb_1")
LB_RB = ("lb", "rb_0", "rb_1")


highest = lax.Precision.HIGHEST
epsilon = 1e-06


def sent_to_all(x, axis):
    size = lax.axis_size(axis)
    return lax.all_to_all(jnp.broadcast_to(x[None], (size, *x.shape)), axis, 0, 0, tiled=True)


def taken_together(x, axis):
    return sent_to_all(x, axis).sum(axis=0)


def in_order(tiles, dim):
    lengths = list(tiles.shape[1:])
    lengths[dim] *= tiles.shape[0]
    return jnp.moveaxis(tiles, 0, dim).reshape(lengths)


def gathered_copies(x, axis, dim):
    return in_order(sent_to_all(x, axis), dim)


def in_blocks(x, dim, size):
    lengths = x.shape
    tiles = x.reshape(*lengths[:dim], size, lengths[dim] // size, *lengths[dim + 1 :])
    return jnp.moveaxis(tiles, dim, 0)


def summed_on_arrival(x, axis, dim):
    tiles = in_blocks(x, dim, lax.axis_size(axis))
    arrived = lax.all_to_all(tiles, axis, split_axis=0, concat_axis=0, tiled=True)
    return arrived.sum(axis=0)


def by_axis(x, axes):
    return functools.reduce(lax.psum, axes, x)


def lowest_pair(matrix):
    matrix_order = matrix.shape[0]
    vectors = jnp.eye(matrix_order, dtype=jnp.float32)
    positions = jnp.arange(matrix_order, dtype=jnp.int32)
    for rounds in range(SWEEPS):
        for first_row in range(matrix_order):
            for second_row in range(first_row + 1, matrix_order):
                rotation_angle = 0.5 * jnp.arctan2(
                    2.0 * matrix[first_row, second_row],
                    matrix[second_row, second_row] - matrix[first_row, first_row],
                )
                cosine = jnp.cos(rotation_angle)
                sine_value = jnp.sin(rotation_angle)
                first_mask = positions == first_row
                second_mask = positions == second_row
                first_col = matrix[:, first_row : first_row + 1]
                second_col = matrix[:, second_row : second_row + 1]
                matrix = jnp.where(
                    first_mask[None, :],
                    cosine * first_col - sine_value * second_col,
                    jnp.where(
                        second_mask[None, :], sine_value * first_col + cosine * second_col, matrix
                    ),
                )
                first_line = matrix[first_row : first_row + 1, :]
                second_line = matrix[second_row : second_row + 1, :]
                matrix = jnp.where(
                    first_mask[:, None],
                    cosine * first_line - sine_value * second_line,
                    jnp.where(
                        second_mask[:, None], sine_value * first_line + cosine * second_line, matrix
                    ),
                )
                first_vec = vectors[:, first_row : first_row + 1]
                second_vec = vectors[:, second_row : second_row + 1]
                vectors = jnp.where(
                    first_mask[None, :],
                    cosine * first_vec - sine_value * second_vec,
                    jnp.where(
                        second_mask[None, :], sine_value * first_vec + cosine * second_vec, vectors
                    ),
                )
    values = jnp.diagonal(matrix)
    chosen = (positions == jnp.argmin(values)).astype(jnp.float32)
    ritz_value = jnp.sum(values * chosen)
    weights = jnp.sum(vectors * chosen[None, :], axis=1)
    weights = jnp.where(weights[0] < 0.0, -weights, weights)
    return (ritz_value, weights)


def dense_operator(operator_blocks, operator_pairs, levels):
    symmetric = 0.5 * (operator_blocks + jnp.swapaxes(operator_blocks, 1, 2))
    indices = jnp.arange(levels, dtype=jnp.int32)
    left_hot = (operator_pairs[:, 0:1] == indices[None, :]).astype(jnp.float32)
    right_hot = (operator_pairs[:, 1:2] == indices[None, :]).astype(jnp.float32)
    return jnp.einsum("nw,nv,nts->wvts", left_hot, right_hot, symmetric, precision=highest)


def contract_right(vector_rows, right_matrix, local_operator):
    row_count, physical, window = vector_rows.shape
    levels = local_operator.shape[1]
    mixed = jnp.dot(
        vector_rows.reshape(row_count * physical, window),
        right_matrix,
        preferred_element_type=jnp.float32,
    )
    mixed = mixed.reshape(row_count, physical, levels, window)
    return jnp.einsum("kvts,nsvb->kntb", local_operator, mixed, precision=highest).astype(
        jnp.bfloat16
    )


def combine(members, weights):
    total = weights[0] * members[0]
    for member_index in range(1, len(members)):
        total = total + weights[member_index] * members[member_index]
    return total


def per_device(initial_guess, left_environment, right_environment, operator_blocks, operator_pairs):
    own_rows, physical, window = initial_guess.shape
    levels = right_environment.shape[1]
    local_levels = left_environment.shape[0]
    block_rows = left_environment.shape[1] * left_environment.shape[3]
    contracted = left_environment.shape[4]
    total_count = own_rows * physical * window * lax.axis_size("lb") * lax.axis_size(RB)
    left_index = lax.axis_index("lb")
    right_index = lax.axis_index(RB)
    level_index = lax.axis_index("wa")
    operator = dense_operator(operator_blocks, operator_pairs, levels)
    local_operator = lax.dynamic_slice_in_dim(operator, level_index * local_levels, local_levels, 0)
    left_matrix = left_environment.reshape(local_levels, block_rows, contracted)
    right_matrix = right_environment.reshape(window, levels * window)
    own_block = lax.dynamic_slice_in_dim(left_environment, left_index, 1, 1)
    own_block = lax.dynamic_slice_in_dim(own_block, right_index * own_rows, own_rows, 4)
    own_block = own_block.reshape(local_levels, own_rows, own_rows)
    left_diag = jnp.diagonal(own_block, axis1=1, axis2=2).astype(jnp.float32)
    operator_diag = jnp.diagonal(local_operator, axis1=2, axis2=3)
    right_diag = jnp.diagonal(right_environment, axis1=0, axis2=2).astype(jnp.float32)
    diagonal_part = jnp.einsum(
        "kr,kvs,vb->rsb", left_diag, operator_diag, right_diag, precision=highest
    )
    diagonal_values = taken_together(diagonal_part, "wa")

    def contract_piece(shard_rows):
        return contract_right(shard_rows, right_matrix, local_operator)

    def apply_hamiltonian(vector):
        vector_bf = vector.astype(jnp.bfloat16)
        inner_terms = contract_piece(gathered_copies(vector_bf, RB, 0))
        partial_value = summed_on_arrival(
            jnp.einsum(
                "kma,katb->mtb", left_matrix, inner_terms, preferred_element_type=jnp.float32
            ),
            "lb",
            0,
        )
        return taken_together(partial_value, "wa")

    def subspace_entries(members, image):
        local_sums = jnp.stack([jnp.sum(member * image) for member in members])
        return by_axis(local_sums, LB_RB) / total_count

    start_vector = initial_guess.astype(jnp.float32)
    start_norm = by_axis(jnp.sum(start_vector * start_vector), LB_RB) / total_count
    basis = [start_vector * lax.rsqrt(start_norm + epsilon)]
    images = [apply_hamiltonian(basis[0])]
    subspace = jnp.zeros((ITERS + 1, ITERS + 1), jnp.float32)
    subspace = subspace.at[0, 0].set(subspace_entries(basis, images[0])[0])
    for step_index in range(ITERS):
        filled = step_index + 1
        ritz_value, weights = lowest_pair(subspace[:filled, :filled])
        ritz_now = combine(basis, weights)
        residual_now = combine(images, weights) - ritz_value * ritz_now
        correction = residual_now / (jnp.abs(diagonal_values - ritz_value) + 1.0)
        local_correlations = jnp.stack([jnp.sum(member * correction) for member in basis])
        correlation_sums, square_sum = (
            by_axis(local_correlations, LB_RB),
            by_axis(jnp.sum(correction * correction), LB_RB),
        )
        correlation_values = correlation_sums / total_count
        correction = correction - combine(basis, correlation_values)
        squared = square_sum / total_count - jnp.sum(correlation_values * correlation_values)
        new_vector = correction * lax.rsqrt(squared + epsilon)
        new_image = apply_hamiltonian(new_vector)
        basis.append(new_vector)
        images.append(new_image)
        row_values = subspace_entries(basis, new_image)
        subspace = (
            subspace.at[filled, : filled + 1]
            .set(row_values)
            .at[: filled + 1, filled]
            .set(row_values)
        )
    ritz_value, weights = lowest_pair(subspace)
    ritz_vector = combine(basis, weights)
    residual = combine(images, weights) - ritz_value * ritz_vector
    return (ritz_vector, residual)


def solution(mesh):
    split = Mesh(
        mesh.devices.reshape(mesh.shape["lb"], 4, 4, mesh.shape["wa"]), ("lb", "rb_0", "rb_1", "wa")
    )
    in_specs = (P(LB_RB, None, None), P("wa", None, RB, None, "lb"), P(), P(), P())
    out_specs = (P(LB_RB, None, None), P(LB_RB, None, None))
    return jax.shard_map(
        per_device, mesh=split, in_specs=in_specs, out_specs=out_specs, check_vma=False
    )
```

profile of v0, /device:TPU:1, one launch (start us, length us, event | category | flops | bytes accessed | tf_op | source)
XLA Modules:
  0.0 914.2 jit_solution(16153142734862492179)
XLA Ops:
  2.1 17.9 %psum.231 = f32[]{:T(128)} all-reduce(f32[]{:T(128)} %fusion.93), channel_id=1, replica_groups=mesh['lb'=8,'rb_0'=4,'rb_1'=4,'wa'=2] {'lb'}, use_global_device_ids=true, to_apply=%region_1.2 | all-reduce | flops 1 | bytes 8 | tf_op jit(solution)/shard_map/psum | solution.py:51
  29.1 9.6 %psum.233 = f32[]{:T(128)} all-reduce(f32[]{:T(128)} %psum.232), channel_id=1, replica_groups=mesh['lb'=8,'rb_0'=4,'rb_1'=4,'wa'=2] {'rb_1'}, use_global_device_ids=true, to_apply=%region_3.4 | all-reduce | flops 1 | bytes 8 | tf_op jit(solution)/shard_map/psum | solution.py:51
  59.3 29.3 %fusion.24 = bf16[4,1024,4,128]{3,2,0,1:T(4,128)(2,1)S(1)} fusion(f32[1024,4,8,128,1]{3,0,2,1,4:T(8,128)S(1)} %convolution_bitcast_fusion.3, f32[4,8,4,4]{1,2,3,0:T(4,128)S(1)} %copy.123), kind=kOutput, calls=%fused_computation.30 | convolution fusion | flops 807403520 | bytes 20973568 | tf_op jit(solution)/shard_map/kvts,nsvb->kntb/dot_general | solution.py:121
  105.0 11.2 %all-to-all-done.1 = f32[8,64,4,128]{3,1,2,0:T(8,128)S(1)} async-done(((f32[8,64,4,128]{3,1,2,0:T(8,128)}), f32[8,64,4,128]{3,1,2,0:T(8,128)S(1)}, u32[]{:S(2)}, u32[]{:S(2)}) %all-to-all-start.1) | async-done | bytes 1048608 | tf_op jit(solution)/shard_map/all_to_all | solution.py:46
  116.3 13.4 %all_to_all.65 = f32[2,64,4,128]{3,1,2,0:T(8,128)S(1)} all-to-all(f32[2,64,4,128]{3,1,2,0:T(8,128)S(1)} %broadcast_in_dim.6365), channel_id=1, replica_groups=mesh['lb'=8,'rb_0'=4,'rb_1'=4,'wa'=2] {'wa'}, dimensions={0} | all-to-all | bytes 524288 | tf_op jit(solution)/shard_map/all_to_all | solution.py:21
  130.4 11.4 %psum.234 = f32[1]{0:T(128)} all-reduce(f32[1]{0:T(128)} %bitcast.24), channel_id=1, replica_groups=mesh['lb'=8,'rb_0'=4,'rb_1'=4,'wa'=2] {'lb'}, use_global_device_ids=true, to_apply=%region_7.8 | all-reduce | flops 1 | bytes 8 | tf_op jit(solution)/shard_map/psum | solution.py:51
  165.4 13.3 %all-reduce.3 = (f32[]{:T(128)}, f32[1]{0:T(128)}) all-reduce(f32[]{:T(128)} %get-tuple-element.111, f32[1]{0:T(128)} %bitcast.36), channel_id=1, replica_groups=mesh['lb'=8,'rb_0'=4,'rb_1'=4,'wa'=2] {'lb'}, use_global_device_ids=true, to_apply=%region_16.17 | all-reduce | flops 2 | bytes 16 | tf_op jit(solution)/shard_map/psum | solution.py:51
  197.0 14.4 %all_to_all.66 = bf16[16,64,4,128]{3,1,2,0:T(8,128)(2,1)S(1)} all-to-all(bf16[16,64,4,128]{3,1,2,0:T(8,128)(2,1)S(1)} %broadcast_in_dim.6367), channel_id=1, replica_groups=mesh['lb'=8,'rb_0'=4,'rb_1'=4,'wa'=2] {'rb_0','rb_1'}, dimensions={0} | all-to-all | bytes 2097152 | tf_op jit(solution)/shard_map/all_to_all | solution.py:21
  213.8 29.5 %fusion.27 = bf16[4,1024,4,128]{3,2,0,1:T(4,128)(2,1)S(1)} fusion(f32[1024,4,8,128,1]{3,0,2,1,4:T(8,128)S(1)} %convolution_bitcast_fusion.2, f32[4,8,4,4]{1,2,3,0:T(4,128)S(1)} %copy.123), kind=kOutput, calls=%fused_computation.31 | convolution fusion | flops 807403520 | bytes 20973568 | tf_op jit(solution)/shard_map/kvts,nsvb->kntb/dot_general | solution.py:121
  251.8 17.0 %all-to-all-done.5 = f32[8,64,4,128]{3,1,2,0:T(8,128)S(1)} async-done(((f32[8,64,4,128]{3,1,2,0:T(8,128)}), f32[8,64,4,128]{3,1,2,0:T(8,128)S(1)}, u32[]{:S(2)}, u32[]{:S(2)}) %all-to-all-start.5) | async-done | bytes 1048608 | tf_op jit(solution)/shard_map/all_to_all | solution.py:46
  268.9 18.8 %all_to_all.67 = f32[2,64,4,128]{3,1,2,0:T(8,128)S(1)} all-to-all(f32[2,64,4,128]{3,1,2,0:T(8,128)S(1)} %broadcast_in_dim.6368), channel_id=1, replica_groups=mesh['lb'=8,'rb_0'=4,'rb_1'=4,'wa'=2] {'wa'}, dimensions={0} | all-to-all | bytes 524288 | tf_op jit(solution)/shard_map/all_to_all | solution.py:21
  289.8 10.9 %psum.243 = f32[2]{0:T(128)S(1)} all-reduce(f32[2]{0:T(128)S(1)} %pad_maximum_fusion), channel_id=1, replica_groups=mesh['lb'=8,'rb_0'=4,'rb_1'=4,'wa'=2] {'lb'}, use_global_device_ids=true, to_apply=%region_23.24 | all-reduce | flops 2 | bytes 16 | tf_op jit(solution)/shard_map/psum | solution.py:51
  349.3 12.8 %all-reduce.2 = (f32[]{:T(128)}, f32[2]{0:T(128)S(1)}) all-reduce(f32[]{:T(128)} %get-tuple-element.106, f32[2]{0:T(128)S(1)} %pad_maximum_fusion.1), channel_id=1, replica_groups=mesh['lb'=8,'rb_0'=4,'rb_1'=4,'wa'=2] {'lb'}, use_global_device_ids=true, to_apply=%region_35.36 | all-reduce | flops 3 | bytes 24 | tf_op jit(solution)/shard_map/psum | solution.py:51
  381.3 14.4 %all_to_all.68 = bf16[16,64,4,128]{3,1,2,0:T(8,128)(2,1)S(1)} all-to-all(bf16[16,64,4,128]{3,1,2,0:T(8,128)(2,1)S(1)} %broadcast_in_dim.6469), channel_id=1, replica_groups=mesh['lb'=8,'rb_0'=4,'rb_1'=4,'wa'=2] {'rb_0','rb_1'}, dimensions={0} | all-to-all | bytes 2097152 | tf_op jit(solution)/shard_map/all_to_all | solution.py:21
  398.1 29.5 %fusion.30 = bf16[4,1024,4,128]{3,2,0,1:T(4,128)(2,1)S(1)} fusion(f32[1024,4,8,128,1]{3,0,2,1,4:T(8,128)S(1)} %convolution_bitcast_fusion.1, f32[4,8,4,4]{1,2,3,0:T(4,128)S(1)} %copy.123), kind=kOutput, calls=%fused_computation.32 | convolution fusion | flops 807403520 | bytes 20973568 | tf_op jit(solution)/shard_map/kvts,nsvb->kntb/dot_general | solution.py:121
  436.8 16.4 %all-to-all-done.8 = f32[8,64,4,128]{3,1,2,0:T(8,128)S(1)} async-done(((f32[8,64,4,128]{3,1,2,0:T(8,128)}), f32[8,64,4,128]{3,1,2,0:T(8,128)S(1)}, u32[]{:S(2)}, u32[]{:S(2)}) %all-to-all-start.8) | async-done | bytes 1048608 | tf_op jit(solution)/shard_map/all_to_all | solution.py:46
  453.3 23.4 %all_to_all.69 = f32[2,64,4,128]{3,1,2,0:T(8,128)S(1)} all-to-all(f32[2,64,4,128]{3,1,2,0:T(8,128)S(1)} %broadcast_in_dim.6470), channel_id=1, replica_groups=mesh['lb'=8,'rb_0'=4,'rb_1'=4,'wa'=2] {'wa'}, dimensions={0} | all-to-all | bytes 524288 | tf_op jit(solution)/shard_map/all_to_all | solution.py:21
  479.5 10.9 %psum.252 = f32[3]{0:T(128)S(1)} all-reduce(f32[3]{0:T(128)S(1)} %pad_maximum_fusion.2), channel_id=1, replica_groups=mesh['lb'=8,'rb_0'=4,'rb_1'=4,'wa'=2] {'lb'}, use_global_device_ids=true, to_apply=%region_44.45 | all-reduce | flops 3 | bytes 24 | tf_op jit(solution)/shard_map/psum | solution.py:51
  594.5 12.8 %all-reduce.1 = (f32[]{:T(128)}, f32[3]{0:T(128)S(1)}) all-reduce(f32[]{:T(128)} %get-tuple-element.99, f32[3]{0:T(128)S(1)} %pad_maximum_fusion.3), channel_id=1, replica_groups=mesh['lb'=8,'rb_0'=4,'rb_1'=4,'wa'=2] {'lb'}, use_global_device_ids=true, to_apply=%region_58.59 | all-reduce | flops 4 | bytes 32 | tf_op jit(solution)/shard_map/psum | solution.py:51
  627.3 14.6 %all_to_all.70 = bf16[16,64,4,128]{3,1,2,0:T(8,128)(2,1)S(1)} all-to-all(bf16[16,64,4,128]{3,1,2,0:T(8,128)(2,1)S(1)} %broadcast_in_dim.6765), channel_id=1, replica_groups=mesh['lb'=8,'rb_0'=4,'rb_1'=4,'wa'=2] {'rb_0','rb_1'}, dimensions={0} | all-to-all | bytes 2097152 | tf_op jit(solution)/shard_map/all_to_all | solution.py:21
  644.3 29.1 %fusion.33 = bf16[4,1024,4,128]{3,2,0,1:T(4,128)(2,1)S(1)} fusion(f32[1024,4,8,128,1]{3,0,2,1,4:T(8,128)S(1)} %convolution_bitcast_fusion, f32[4,8,4,4]{1,2,3,0:T(4,128)S(1)} %copy.123), kind=kOutput, calls=%fused_computation.33 | convolution fusion | flops 807403520 | bytes 20973568 | tf_op jit(solution)/shard_map/kvts,nsvb->kntb/dot_general | solution.py:121
  676.6 20.9 %all_to_all.71 = f32[8,64,4,128]{3,1,2,0:T(8,128)S(1)} all-to-all(f32[8,64,4,128]{3,1,2,0:T(8,128)S(1)} %copy.154), channel_id=1, replica_groups=mesh['lb'=8,'rb_0'=4,'rb_1'=4,'wa'=2] {'lb'}, dimensions={0} | all-to-all | bytes 2097152 | tf_op jit(solution)/shard_map/all_to_all | solution.py:46
  697.6 23.2 %all_to_all.72 = f32[2,64,4,128]{3,1,2,0:T(8,128)S(1)} all-to-all(f32[2,64,4,128]{3,1,2,0:T(8,128)S(1)} %broadcast_in_dim.6766), channel_id=1, replica_groups=mesh['lb'=8,'rb_0'=4,'rb_1'=4,'wa'=2] {'wa'}, dimensions={0} | all-to-all | bytes 524288 | tf_op jit(solution)/shard_map/all_to_all | solution.py:21
  724.2 10.9 %psum.261 = f32[4]{0:T(128)S(1)} all-reduce(f32[4]{0:T(128)S(1)} %pad_maximum_fusion.4), channel_id=1, replica_groups=mesh['lb'=8,'rb_0'=4,'rb_1'=4,'wa'=2] {'lb'}, use_global_device_ids=true, to_apply=%region_68.69 | all-reduce | flops 4 | bytes 32 | tf_op jit(solution)/shard_map/psum | solution.py:51
  (647 shorter events, 312.6 us)
Async XLA Ops:
  41.4 15.4 %all-to-all-start = ((bf16[16,64,4,128]{3,1,2,0:T(8,128)(2,1)}), bf16[16,64,4,128]{3,1,2,0:T(8,128)(2,1)S(1)}, u32[]{:S(2)}, u32[]{:S(2)}) async-start(bf16[16,64,4,128]{3,1,2,0:T(8,128)(2,1)} %broadcast_in_dim.6364), calls=%async_computation | async-start | bytes 2097152 | tf_op jit(solution)/shard_map/all_to_all | solution.py:21
  59.3 29.3 %copy-start.2 = (bf16[4,8,1,64,1024]{4,3,2,1,0:T(8,128)(2,1)S(1)}, bf16[4,8,1,64,1024]{4,3,2,1,0:T(8,128)(2,1)}, u32[]{:S(2)}) copy-start(bf16[4,8,1,64,1024]{4,3,2,1,0:T(8,128)(2,1)} %param.20) | copy-start | bytes 12582916
  91.4 5.1 copy-start.1
  92.8 23.5 %all-to-all-start.1 = ((f32[8,64,4,128]{3,1,2,0:T(8,128)}), f32[8,64,4,128]{3,1,2,0:T(8,128)S(1)}, u32[]{:S(2)}, u32[]{:S(2)}) async-start(f32[8,64,4,128]{3,1,2,0:T(8,128)} %copy.126), calls=%async_computation.1 | async-start | bytes 2097152 | tf_op jit(solution)/shard_map/all_to_all | solution.py:46
  96.5 33.2 %copy-start = (bf16[64,4,128]{2,1,0:T(4,128)(2,1)S(1)}, bf16[64,4,128]{2,1,0:T(4,128)(2,1)}, u32[]{:S(2)}) copy-start(bf16[64,4,128]{2,1,0:T(4,128)(2,1)} %param.19) | copy-start | bytes 196612
  142.5 14.7 %all-to-all-start.3 = ((f32[2,64,4,128]{3,1,2,0:T(8,128)}), f32[2,64,4,128]{3,1,2,0:T(8,128)S(1)}, u32[]{:S(2)}, u32[]{:S(2)}) async-start(f32[2,64,4,128]{3,1,2,0:T(8,128)} %broadcast_in_dim.6366), calls=%async_computation.3 | async-start | bytes 524288 | tf_op jit(solution)/shard_map/all_to_all | solution.py:21
  213.8 29.5 %copy-start.3 = (bf16[4,8,1,64,1024]{4,3,2,1,0:T(8,128)(2,1)S(1)}, bf16[4,8,1,64,1024]{4,3,2,1,0:T(8,128)(2,1)}, u32[]{:S(2)}) copy-start(bf16[4,8,1,64,1024]{4,3,2,1,0:T(8,128)(2,1)} %param.20) | copy-start | bytes 12582916
  247.5 21.3 %all-to-all-start.5 = ((f32[8,64,4,128]{3,1,2,0:T(8,128)}), f32[8,64,4,128]{3,1,2,0:T(8,128)S(1)}, u32[]{:S(2)}, u32[]{:S(2)}) async-start(f32[8,64,4,128]{3,1,2,0:T(8,128)} %copy.138), calls=%async_computation.5 | async-start | bytes 2097152 | tf_op jit(solution)/shard_map/all_to_all | solution.py:46
  398.1 29.6 %copy-start.4 = (bf16[4,8,1,64,1024]{4,3,2,1,0:T(8,128)(2,1)S(1)}, bf16[4,8,1,64,1024]{4,3,2,1,0:T(8,128)(2,1)}, u32[]{:S(2)}) copy-start(bf16[4,8,1,64,1024]{4,3,2,1,0:T(8,128)(2,1)} %param.20) | copy-start | bytes 12582916
  430.5 5.7 copy-start.6
  431.9 21.3 %all-to-all-start.8 = ((f32[8,64,4,128]{3,1,2,0:T(8,128)}), f32[8,64,4,128]{3,1,2,0:T(8,128)S(1)}, u32[]{:S(2)}, u32[]{:S(2)}) async-start(f32[8,64,4,128]{3,1,2,0:T(8,128)} %copy.146), calls=%async_computation.8 | async-start | bytes 2097152 | tf_op jit(solution)/shard_map/all_to_all | solution.py:46
  644.3 29.2 %copy-start.5 = (bf16[4,8,1,64,1024]{4,3,2,1,0:T(8,128)(2,1)S(1)}, bf16[4,8,1,64,1024]{4,3,2,1,0:T(8,128)(2,1)}, u32[]{:S(2)}) copy-start(bf16[4,8,1,64,1024]{4,3,2,1,0:T(8,128)(2,1)} %param.20) | copy-start | bytes 12582916
where the time goes:
time: 928 us; the launch traced here: 914 us
  blocking collectives  362 us (39%)
  between operations  186 us (20%)
  matrix products  140 us (15%)
  local copies, waits for them, and re-layouts  83.2 us (9%)
  other arithmetic  69 us (7%)
  waiting for transfers between devices  53 us (6%)
  starting transfers between devices  21.5 us (2%)
    psum x24, blocking collectives, by_axis(): return functools.reduce(lax.psum, axes, x)  219 us
    all_to_all x7, blocking collectives, sent_to_all(): lax.all_to_all(jnp.broadcast_to(x[None], (size, *x.shape)), axis, 0, 0, t...  122 us
    dot_general x4, matrix products, contract_right(): jnp.einsum('kvts,nsvb->kntb', local_operator, mixed, precision=highest)  118 us
    slice x80, local copies, waits for them, and re-layouts, lowest_pair(): matrix[first_row, first_row]  53.7 us
    all_to_all x3, waiting for transfers between devices, summed_on_arrival(): lax.all_to_all(tiles, axis, split_axis=0, concat_axis=0, tiled=True)  44.7 us
    all_to_all x1, blocking collectives, summed_on_arrival(): lax.all_to_all(tiles, axis, split_axis=0, concat_axis=0, tiled=True)  20.9 us
  transfers between devices with their start and end apart: 5, of which 4 were waited for; matrix products, arithmetic and copies ran while one was open for 2% of the time, Pallas kernels for 0%

commit v1 on v0

v1 whole, which is shorter than its diff:
```python
import functools

import jax
import jax.numpy as jnp
from jax import lax
from jax.experimental import pallas as pl
from jax.experimental.pallas import tpu as pltpu
from jax.sharding import PartitionSpec as P

ITERS = 3
SWEEPS = 8
STEPS = ITERS + 1
TILE = (8, 128)
LB_RB = ("lb", "rb")
MESH_ID = pl.DeviceIdType.MESH

highest = lax.Precision.HIGHEST
epsilon = 1e-06


def rotate(matrix, vectors, p, q, order):
    y = 2.0 * matrix[p][q]
    x = matrix[q][q] - matrix[p][p]
    square = x * x + y * y
    usable = square > 0.0
    inverse = lax.rsqrt(jnp.where(usable, square, 1.0))
    half_sum = 0.5 + 0.5 * jnp.abs(x * inverse)
    inverse_large = lax.rsqrt(half_sum)
    large = half_sum * inverse_large
    small = 0.5 * jnp.abs(y * inverse) * inverse_large
    forward = x >= 0.0
    cosine = jnp.where(usable, jnp.where(forward, large, small), 1.0)
    sine = jnp.where(usable, jnp.where(forward, small, large), 0.0)
    sine = jnp.where(y < 0.0, -sine, sine)
    m_pp, m_qq, m_pq = matrix[p][p], matrix[q][q], matrix[p][q]
    cc, ss, cs = cosine * cosine, sine * sine, cosine * sine
    cross = 2.0 * cs * m_pq
    matrix[p][p] = cc * m_pp - cross + ss * m_qq
    matrix[q][q] = ss * m_pp + cross + cc * m_qq
    matrix[p][q] = matrix[q][p] = jnp.zeros_like(m_pq)
    for i in range(order):
        if i != p and i != q:
            a, b = matrix[i][p], matrix[i][q]
            matrix[i][p] = matrix[p][i] = cosine * a - sine * b
            matrix[i][q] = matrix[q][i] = sine * a + cosine * b
        a, b = vectors[i][p], vectors[i][q]
        vectors[i][p] = cosine * a - sine * b
        vectors[i][q] = sine * a + cosine * b


def lowest(entries, order):
    if order == 1:
        return entries[0][0], [jnp.ones(TILE, jnp.float32)]
    scale = jnp.abs(entries[0][0])
    for i in range(order):
        for j in range(i, order):
            scale = jnp.maximum(scale, jnp.abs(entries[i][j]))
    inverse = 1.0 / jnp.where(scale > 0.0, scale, 1.0)
    flat = [entries[i][j] * inverse for i in range(order) for j in range(order)]
    flat += [jnp.full(TILE, 1.0 if i == j else 0.0, jnp.float32) for i in range(order) for j in range(order)]

    def sweep(_, flat):
        matrix = [list(flat[i * order : (i + 1) * order]) for i in range(order)]
        base = order * order
        vectors = [list(flat[base + i * order : base + (i + 1) * order]) for i in range(order)]
        for p in range(order):
            for q in range(p + 1, order):
                rotate(matrix, vectors, p, q, order)
        return tuple(v for row in matrix + vectors for v in row)

    flat = lax.fori_loop(0, 1 if order == 2 else SWEEPS, sweep, tuple(flat))
    matrix = [flat[i * order : (i + 1) * order] for i in range(order)]
    base = order * order
    vectors = [flat[base + i * order : base + (i + 1) * order] for i in range(order)]
    best = matrix[0][0]
    weights = [vectors[i][0] for i in range(order)]
    for j in range(1, order):
        less = matrix[j][j] < best
        best = jnp.where(less, matrix[j][j], best)
        weights = [jnp.where(less, vectors[i][j], weights[i]) for i in range(order)]
    negative = weights[0] < 0.0
    weights = [jnp.where(negative, -w, w) for w in weights]
    return best * scale, weights


def kernel(
    dims,
    guess_ref,
    right_ref,
    op_ref,
    left_hbm,
    vector_ref,
    residual_ref,
    left,
    mixing,
    right_rows,
    right_by_level,
    gathered,
    column,
    inner,
    image,
    pair_out,
    pair_in,
    block_out,
    block_in,
    diag_parts,
    diag_in,
    basis,
    images,
    tile_out,
    tiles_a,
    tile_mid,
    tiles_b,
    left_sem,
    x_send,
    x_recv,
    f_send,
    f_recv,
    z_send,
    z_recv,
    p_send,
    p_recv,
    s_send,
    s_recv,
    a_send,
    a_recv,
    b_send,
    b_recv,
    d_sems,
    o_sems,
):
    n_lb, n_rb, line, rows, states, window, levels, local_levels = dims
    lines = n_rb // line
    chunk = line * rows
    half_width = states * window // 2
    block_rows = n_lb * rows
    scale = 1.0 / (n_lb * n_rb * rows * states * window)
    z = lax.axis_index("lb")
    me = lax.axis_index("rb")
    half = lax.axis_index("wa")
    other = 1 - half
    my_line = lax.div(me, line)
    f32, bf16 = jnp.float32, jnp.bfloat16

    def remote(src, dst, send, recv, peer):
        return pltpu.make_async_remote_copy(
            src_ref=src, dst_ref=dst, send_sem=send, recv_sem=recv, device_id=peer, device_id_type=MESH_ID
        )

    def drain(region, sem):
        pltpu.make_async_copy(region, region, sem).wait()

    def each(count, body):
        def step(i, carry):
            body(i)
            return carry

        lax.fori_loop(0, count, step, 0)

    def left_copy(i):
        w, q = lax.div(i, lines), lax.rem(i, lines)
        return pltpu.make_async_copy(
            left_hbm.at[w, :, pl.ds(pl.multiple_of(q * chunk, chunk), chunk)],
            left.at[q, :, pl.ds(pl.multiple_of(w * chunk, chunk), chunk)],
            left_sem,
        )

    each(local_levels * lines, lambda i: left_copy(i).start())

    barrier = pltpu.get_barrier_semaphore()

    def greet(peer):
        pl.semaphore_signal(barrier, inc=1, device_id=peer, device_id_type=MESH_ID)

    each(n_rb - 1, lambda j: greet({"rb": lax.rem(me + 1 + j, n_rb)}))
    each(n_lb - 1, lambda j: greet({"lb": lax.rem(z + 1 + j, n_lb)}))
    each(n_lb, lambda j: greet({"lb": lax.rem(z + j, n_lb), "wa": other}))

    def own(it):
        return gathered.at[it, half, pl.ds(pl.multiple_of(me * rows, rows), rows)]

    def hand_out(it, part):
        own(it)[...] = part
        column[it, z] = part

    def start_hand_out(it):
        def to_plane(j):
            remote(own(it), own(it), x_send.at[it], x_recv.at[it, my_line], {"rb": lax.rem(me + 1 + j, n_rb)}).start()

        def to_column(j):
            remote(column.at[it, z], column.at[it, z], z_send.at[it], z_recv.at[it], {"lb": lax.rem(z + 1 + j, n_lb)}).start()

        each(n_rb - 1, to_plane)
        each(n_lb - 1, to_column)

    def own_half(ref):
        return jnp.where(half == 0, ref[:, :half_width], ref[:, half_width:])

    first = own_half(guess_ref)
    hand_out(0, first)
    current = first.astype(f32)
    pl.semaphore_wait(barrier, (n_rb - 1) + (n_lb - 1) + n_lb)
    start_hand_out(0)

    right_rows[...] = right_ref[...].astype(f32).reshape(window * levels, window)
    for v in range(levels):
        right_by_level[v] = right_rows[pl.ds(v, window, stride=levels), :]

    def op_at(w, v, t, s):
        return op_ref[((w * levels + v) * states + t) * states + s]

    def mix_level(w):
        for t in range(states):
            for s in range(t, states):
                tile = op_at(w, 0, t, s) * right_by_level[0]
                for v in range(1, levels):
                    tile = tile + op_at(w, v, t, s) * right_by_level[v]
                tile = tile.astype(bf16)
                for a, b in {(t, s), (s, t)}:
                    mixing[w, a // 2, b * window : (b + 1) * window, (a % 2) * window : (a % 2 + 1) * window] = tile

    each(local_levels, mix_level)

    row_at = lax.broadcasted_iota(jnp.int32, (window, window), 0)
    col_at = lax.broadcasted_iota(jnp.int32, (window, window), 1)
    right_diag = [
        jnp.sum(jnp.where(row_at == col_at, right_by_level[v], 0.0), axis=0, keepdims=True) for v in range(levels)
    ]
    each(local_levels * lines, lambda i: left_copy(i).wait())
    q_own = my_line
    inside = lax.rem(me, line) * rows
    at_row = lax.broadcasted_iota(jnp.int32, (rows, chunk), 0)
    at_col = lax.broadcasted_iota(jnp.int32, (rows, chunk), 1)
    picked = at_col == at_row + inside
    parts = [jnp.zeros((rows, window), f32) for _ in range(states)]
    for w in range(local_levels):
        entries = left[q_own, pl.ds(pl.multiple_of(z * rows, rows), rows), w * chunk : (w + 1) * chunk].astype(f32)
        left_diag = jnp.sum(jnp.where(picked, entries, 0.0), axis=1, keepdims=True)
        for s in range(states):
            along = op_at(w, 0, s, s) * right_diag[0]
            for v in range(1, levels):
                along = along + op_at(w, v, s, s) * right_diag[v]
            parts[s] = parts[s] + left_diag * along
    for s in range(states):
        diag_parts[s // 2, :, (s % 2) * window : (s % 2 + 1) * window] = parts[s]
    diag_copy = remote(diag_parts.at[other], diag_in, d_sems.at[0], d_sems.at[1], {"wa": other})
    diag_copy.start()

    def spread(number):
        piece = jnp.broadcast_to(number[0:1, :], (rows, TILE[1]))
        return jnp.concatenate([piece] * (half_width // TILE[1]), axis=1)

    def lane_sums(value):
        total = jnp.sum(value, axis=0, keepdims=True)
        out = total[:, : TILE[1]]
        for i in range(1, half_width // TILE[1]):
            out = out + total[:, i * TILE[1] : (i + 1) * TILE[1]]
        return out

    def chunk_rows(q):
        return pl.ds(pl.multiple_of(q * chunk, chunk), chunk)

    def line_at(i):
        if lines == 4:
            i = i + lax.div(i, 2) - 2 * lax.div(i, 3)
        return lax.rem(my_line + i, lines)

    def forward(it, q):
        region = gathered.at[it, half, chunk_rows(q)]
        return remote(region, region, f_send.at[it, q], f_recv.at[it, q], {"wa": other})

    def multiply(it, q):
        x = jnp.concatenate([gathered[it, 0, chunk_rows(q), :], gathered[it, 1, chunk_rows(q), :]], axis=1)

        def to_inner(i):
            h, w = lax.div(i, local_levels), lax.rem(i, local_levels)
            inner[h, chunk_rows(w), :] = jnp.dot(x, mixing[w, h], preferred_element_type=f32).astype(bf16)

        each(2 * local_levels, to_inner)

        def to_image(h):
            image[h] += jnp.dot(left[q], inner[h], preferred_element_type=f32)

        each(2, to_image)

    def apply(it, member):
        image[...] = jnp.zeros_like(image)
        drain(gathered.at[it, half, pl.ds(0, chunk - rows)], x_recv.at[it, my_line])
        forward(it, my_line).start()

        def one_line(i):
            @pl.when(i < lines - 1)
            def _():
                q = line_at(i + 1)
                drain(gathered.at[it, half, chunk_rows(q)], x_recv.at[it, q])
                forward(it, q).start()

            q = line_at(i)
            drain(gathered.at[it, other, chunk_rows(q)], f_recv.at[it, q])
            multiply(it, q)

        each(lines, one_line)

        pair_out[it] = image[other].astype(bf16)
        pair = remote(pair_out.at[it], pair_in.at[it], p_send.at[it], p_recv.at[it], {"wa": other})
        pair.start()
        drain(column.at[it, pl.ds(0, n_lb - 1)], z_recv.at[it])
        sums = [lane_sums(member * member)]
        sums += [lane_sums(basis[j] * member) for j in range(it)]
        sums += [lane_sums(images[j] * member) for j in range(it)]
        pair.wait_recv()
        product = jnp.zeros((1, TILE[1]), f32)
        mine = None
        for b in range(n_lb):
            summed = image[half, b * rows : (b + 1) * rows, :] + pair_in[it, b * rows : (b + 1) * rows, :].astype(f32)
            image[half, b * rows : (b + 1) * rows, :] = summed
            block_out[it, b] = summed.astype(bf16)
            product = product + lane_sums(summed * column[it, b].astype(f32))

        def to_block(j):
            b = lax.rem(z + 1 + j, n_lb)
            remote(block_out.at[it, b], block_in.at[it, z], s_send.at[it], s_recv.at[it], {"lb": b}).start()

        each(n_lb - 1, to_block)

        row = lax.broadcasted_iota(jnp.int32, TILE, 0)
        tile = jnp.zeros(TILE, f32)
        for i, value in enumerate([product] + sums):
            tile = jnp.where(row == i, jnp.broadcast_to(value, TILE), tile)
        totals = add_up(it, tile)

        drain(block_in.at[it, pl.ds(0, n_lb - 1)], s_recv.at[it])
        total = image[half, pl.ds(pl.multiple_of(z * rows, rows), rows), :]
        for j in range(1, n_lb):
            total = total + block_in[it, lax.rem(z + j, n_lb)].astype(f32)
        return total, totals

    def add_up(it, tile):
        slot = z * 2 + half
        tiles_a[it, slot] = tile
        tile_out[it] = tile

        def along(j):
            remote(tile_out.at[it], tiles_a.at[it, slot], a_send.at[it], a_recv.at[it], {"lb": lax.rem(z + 1 + j, n_lb)}).start()

        def across(j):
            remote(
                tile_out.at[it], tiles_a.at[it, slot], a_send.at[it], a_recv.at[it],
                {"lb": lax.rem(z + j, n_lb), "wa": other},
            ).start()

        each(n_lb - 1, along)
        each(n_lb, across)
        drain(tiles_a.at[it, pl.ds(0, 2 * n_lb - 1)], a_recv.at[it])
        tile = tiles_a[it, 0]
        for j in range(1, 2 * n_lb):
            tile = tile + tiles_a[it, j]
        tiles_b[it, me] = tile
        tile_mid[it] = tile

        def plane(j):
            remote(tile_mid.at[it], tiles_b.at[it, me], b_send.at[it], b_recv.at[it], {"rb": lax.rem(me + 1 + j, n_rb)}).start()

        each(n_rb - 1, plane)
        drain(tiles_b.at[it, pl.ds(0, n_rb - 1)], b_recv.at[it])
        tile = tiles_b[it, 0]
        for j in range(1, n_rb):
            tile = tile + tiles_b[it, j]
        tile = jnp.broadcast_to(jnp.sum(tile, axis=1, keepdims=True), TILE) * scale
        return [jnp.broadcast_to(tile[i : i + 1, :], TILE) for i in range(2 + 2 * it)]

    entries = [[None] * STEPS for _ in range(STEPS)]
    diagonal = None
    for it in range(STEPS):
        applied, totals = apply(it, current)
        energy, square = totals[0], totals[1]
        overlaps, crossed = totals[2 : 2 + it], totals[2 + it :]
        norm = square
        for a in overlaps:
            norm = norm - a * a
        inverse = lax.rsqrt(jnp.maximum(norm, 0.0) + epsilon)
        for j in range(it):
            value = crossed[j]
            for i in range(it):
                value = value - overlaps[i] * entries[i][j]
            entries[j][it] = entries[it][j] = inverse * value
            energy = energy - overlaps[j] * (crossed[j] + value)
        entries[it][it] = inverse * inverse * energy
        theta, weights = lowest(entries, it + 1)

        vector, applied_now = current, applied
        for j in range(it):
            a = spread(overlaps[j])
            vector = vector - a * basis[j]
            applied_now = applied_now - a * images[j]
        grow = spread(inverse)
        vector, applied_now = vector * grow, applied_now * grow
        basis[it] = vector
        images[it] = applied_now
        last = spread(weights[it])
        ritz, residual = last * vector, last * applied_now
        for j in range(it):
            a = spread(weights[j])
            ritz = ritz + a * basis[j]
            residual = residual + a * images[j]
        shift = spread(theta)
        residual = residual - shift * ritz
        if it == 0:
            diag_copy.wait()
            diagonal = diag_parts[half] + diag_in[...]
            diag_parts[half] = diagonal
        if it < ITERS:
            current = residual / (jnp.abs(diag_parts[half] - shift) + 1.0)
            hand_out(it + 1, current.astype(bf16))
            start_hand_out(it + 1)

    vector_ref[half] = ritz
    residual_ref[half] = residual
    copies = [
        remote(ref.at[half], ref.at[half], o_sems.at[2 * i], o_sems.at[2 * i + 1], {"wa": other})
        for i, ref in enumerate((vector_ref, residual_ref))
    ]
    for copy in copies:
        copy.start()

    def finish(it):
        drain(gathered.at[it, 0, pl.ds(0, (n_rb - 1) * rows)], x_send.at[it])
        drain(column.at[it, pl.ds(0, n_lb - 1)], z_send.at[it])
        each(lines, lambda q: forward(it, q).wait_send())
        drain(pair_out.at[it], p_send.at[it])
        drain(block_out.at[it, pl.ds(0, n_lb - 1)], s_send.at[it])
        drain(tiles_a.at[it, pl.ds(0, 2 * n_lb - 1)], a_send.at[it])
        drain(tiles_b.at[it, pl.ds(0, n_rb - 1)], b_send.at[it])

    each(STEPS, finish)
    for copy in copies:
        copy.wait()


def dense_operator(operator_blocks, operator_pairs, first_level, local_levels, levels):
    symmetric = 0.5 * (operator_blocks + jnp.swapaxes(operator_blocks, 1, 2))
    count = symmetric.shape[0]
    left_hot = operator_pairs[:, 0][:, None] == first_level + jnp.arange(local_levels, dtype=jnp.int32)[None]
    right_hot = operator_pairs[:, 1][:, None] == jnp.arange(levels, dtype=jnp.int32)[None]
    hot = left_hot[:, :, None, None] & right_hot[:, None, :, None]
    return jnp.sum(jnp.where(hot, symmetric.reshape(count, 1, 1, -1), 0.0), axis=0).reshape(-1)


def per_device(initial_guess, left_environment, right_environment, operator_blocks, operator_pairs):
    rows, states, window = initial_guess.shape
    levels = right_environment.shape[1]
    local_levels, n_lb = left_environment.shape[:2]
    contracted = left_environment.shape[4]
    n_rb = lax.axis_size("rb")
    line = 4 if n_rb == 16 else 2
    lines, chunk = n_rb // line, line * rows
    width, half_width = states * window, states * window // 2
    block_rows = n_lb * rows
    operator = dense_operator(
        operator_blocks, operator_pairs, lax.axis_index("wa") * local_levels, local_levels, levels
    )
    dims = (n_lb, n_rb, line, rows, states, window, levels, local_levels)
    f32, bf16 = jnp.float32, jnp.bfloat16
    dma = pltpu.SemaphoreType.DMA
    vmem = pl.BlockSpec(memory_space=pltpu.VMEM)
    out = jax.ShapeDtypeStruct((2, rows, half_width), f32)
    outs = pl.pallas_call(
        functools.partial(kernel, dims),
        out_shape=(out, out),
        in_specs=[vmem, vmem, pl.BlockSpec(memory_space=pltpu.SMEM), pl.BlockSpec(memory_space=pl.ANY)],
        out_specs=(vmem, vmem),
        scratch_shapes=[
            pltpu.VMEM((lines, block_rows, local_levels * chunk), bf16),
            pltpu.VMEM((local_levels, 2, width, half_width), bf16),
            pltpu.VMEM((window * levels, window), f32),
            pltpu.VMEM((levels, window, window), f32),
            pltpu.VMEM((STEPS, 2, contracted, half_width), bf16),
            pltpu.VMEM((STEPS, n_lb, rows, half_width), bf16),
            pltpu.VMEM((2, local_levels * chunk, half_width), bf16),
            pltpu.VMEM((2, block_rows, half_width), f32),
            pltpu.VMEM((STEPS, block_rows, half_width), bf16),
            pltpu.VMEM((STEPS, block_rows, half_width), bf16),
            pltpu.VMEM((STEPS, n_lb, rows, half_width), bf16),
            pltpu.VMEM((STEPS, n_lb, rows, half_width), bf16),
            pltpu.VMEM((2, rows, half_width), f32),
            pltpu.VMEM((rows, half_width), f32),
            pltpu.VMEM((STEPS, rows, half_width), f32),
            pltpu.VMEM((STEPS, rows, half_width), f32),
            pltpu.VMEM((STEPS, *TILE), f32),
            pltpu.VMEM((STEPS, 2 * n_lb, *TILE), f32),
            pltpu.VMEM((STEPS, *TILE), f32),
            pltpu.VMEM((STEPS, n_rb, *TILE), f32),
            dma(()),
            dma((STEPS,)),
            dma((STEPS, lines)),
            dma((STEPS, lines)),
            dma((STEPS, lines)),
            dma((STEPS,)),
            dma((STEPS,)),
            dma((STEPS,)),
            dma((STEPS,)),
            dma((STEPS,)),
            dma((STEPS,)),
            dma((STEPS,)),
            dma((STEPS,)),
            dma((STEPS,)),
            dma((STEPS,)),
            dma((2,)),
            dma((4,)),
        ],
        compiler_params=pltpu.CompilerParams(collective_id=0, has_side_effects=True),
        name="davidson",
    )(
        initial_guess.reshape(rows, width),
        right_environment,
        operator,
        left_environment.reshape(local_levels, block_rows, contracted),
    )
    return tuple(
        o.reshape(2, rows, states // 2, window).transpose(1, 0, 2, 3).reshape(rows, states, window) for o in outs
    )


def solution(mesh):
    in_specs = (P(LB_RB, None, None), P("wa", None, "rb", None, "lb"), P(), P(), P())
    out_specs = (P(LB_RB, None, None), P(LB_RB, None, None))
    return jax.shard_map(per_device, mesh=mesh, in_specs=in_specs, out_specs=out_specs, check_vma=False)
```

time: 928 us -> 172 us (0.19); the launches traced: 914 us -> 172 us
  blocking collectives: 362 us -> 0 us
  between operations: 186 us -> 0.67 us
  Pallas kernels: 0 us -> 164 us
  matrix products: 140 us -> 0 us
  local copies, waits for them, and re-layouts: 83.2 us -> 6.31 us
  other arithmetic: 69 us -> 1.15 us
  waiting for transfers between devices: 53 us -> 0 us
  starting transfers between devices: 21.5 us -> 0 us
    psum x24 -> x0, blocking collectives: 219 us -> none  [by_axis(): return functools.reduce(lax.psum, axes, x)]
    pallas_call x0 -> x1, Pallas kernels: none -> 164 us  [per_device(): pl.pallas_call(functools.partial(kernel, dims), out_shape=(out, out), in_...]
    all_to_all x8 -> x0, blocking collectives: 143 us -> none  [the longest x7 122 us: sent_to_all(): lax.all_to_all(jnp.broadcast_to(x[None], (size, *x.shape)), axis, 0, 0, t...]
    dot_general x15 -> x0, matrix products: 140 us -> none  [the longest x4 118 us: contract_right(): jnp.einsum('kvts,nsvb->kntb', local_operator, mixed, precision=highest)]
    slice x85 -> x1, local copies, waits for them, and re-layouts: 56.7 us -> 0.76 us  [dense_operator(): operator_pairs[:, 0][:, None]]
    all_to_all x5 -> x0, waiting for transfers between devices: 53 us -> none  [the longest x3 44.7 us: summed_on_arrival(): lax.all_to_all(tiles, axis, split_axis=0, concat_axis=0, tiled=True)]
    all_to_all x5 -> x0, starting transfers between devices: 21.5 us -> none  [the longest x2 10.8 us: sent_to_all(): lax.all_to_all(jnp.broadcast_to(x[None], (size, *x.shape)), axis, 0, 0, t...]
    sub x81 -> x0, other arithmetic: 19.3 us -> none  [the longest x80 16 us: lowest_pair(): cosine * first_line - sine_value * second_line]
  transfers between devices with their start and end apart: 5 -> 0, of which waited for: 4 -> 0; matrix products, arithmetic and copies ran while one was open for 2% -> 0% of each run, Pallas kernels for 0% -> 0%
where the time goes in v1:
time: 172 us
  Pallas kernels  164 us (95%)
  local copies, waits for them, and re-layouts  6.31 us (4%)
    pallas_call x1, Pallas kernels, per_device(): pl.pallas_call(functools.partial(kernel, dims), out_shape=(out, out), in_...  164 us

profile of v1, /device:TPU:1, one launch (start us, length us, event | category | flops | bytes accessed | tf_op | source)
XLA Modules:
  0.0 171.7 jit_solution(3989285582225260323)
XLA Ops:
  0.6 0.8 slice_bitcast_fusion.1
  1.4 0.1 broadcast_compare_fusion
  1.5 0.1 iota_compare_fusion
  1.6 0.1 broadcast_and_fusion
  1.6 0.8 fusion
  2.4 0.1 copy.12
  2.5 0.1 select_reduce_fusion
  2.6 0.7 reshape.89.op_ref
  3.3 1.5 copy.18
  4.8 163.6 %davidson.1 = (f32[2,64,256]{2,1,0:T(8,128)}, f32[2,64,256]{2,1,0:T(8,128)}) custom-call(bf16[64,512]{1,0:T(8,128)(2,1)} %bitcast.21, bf16[128,8,128]{2,1,0:T(8,128)(2,1)} %right_ref.1, f32[512]{0:T(512)} %reshape.89.op_ref, bf16[4,512,1024]{2,1,0:T(8,128)(2,1)} %bitcast.18), custom_call_target="tpu_custom_call" | custom-call | tf_op jit(solution)/shard_map/davidson/pallas_call | solution.py:467
  168.3 1.0 reshape.91
  169.3 0.7 copy.13
  170.0 1.0 reshape.93
  171.0 0.7 copy.14
  (1 shorter events, 0.0 us)

commit v2 on v1

--- a/solution.py
+++ b/solution.py
@@ -185,7 +185,14 @@
 
     def start_hand_out(it):
         def to_plane(j):
-            remote(own(it), own(it), x_send.at[it], x_recv.at[it, my_line], {"rb": lax.rem(me + 1 + j, n_rb)}).start()
+            j = j + 1
+            away, across = lax.div(j, line), lax.rem(me + j, line)
+            if lines == 4:
+                away = 4 * lax.div(away + 3, 4) - (away + lax.div(away, 2) - 2 * lax.div(away, 3))
+            else:
+                away = lines * lax.div(away + lines - 1, lines) - away
+            peer = lax.rem(my_line + away, lines) * line + across
+            remote(own(it), own(it), x_send.at[it], x_recv.at[it, my_line], {"rb": peer}).start()
 
         def to_column(j):
             remote(column.at[it, z], column.at[it, z], z_send.at[it], z_recv.at[it], {"lb": lax.rem(z + 1 + j, n_lb)}).start()
@@ -272,16 +279,13 @@
     def multiply(it, q):
         x = jnp.concatenate([gathered[it, 0, chunk_rows(q), :], gathered[it, 1, chunk_rows(q), :]], axis=1)
 
-        def to_inner(i):
-            h, w = lax.div(i, local_levels), lax.rem(i, local_levels)
-            inner[h, chunk_rows(w), :] = jnp.dot(x, mixing[w, h], preferred_element_type=f32).astype(bf16)
-
-        each(2 * local_levels, to_inner)
-
-        def to_image(h):
+        for h in range(2):
+            for w in range(local_levels):
+                inner[h, w * chunk : (w + 1) * chunk, :] = jnp.dot(
+                    x, mixing[w, h], preferred_element_type=f32
+                ).astype(bf16)
+        for h in range(2):
             image[h] += jnp.dot(left[q], inner[h], preferred_element_type=f32)
-
-        each(2, to_image)
 
     def apply(it, member):
         image[...] = jnp.zeros_like(image)
@@ -321,13 +325,11 @@
             b = lax.rem(z + 1 + j, n_lb)
             remote(block_out.at[it, b], block_in.at[it, z], s_send.at[it], s_recv.at[it], {"lb": b}).start()
 
-        each(n_lb - 1, to_block)
-
         row = lax.broadcasted_iota(jnp.int32, TILE, 0)
         tile = jnp.zeros(TILE, f32)
         for i, value in enumerate([product] + sums):
             tile = jnp.where(row == i, jnp.broadcast_to(value, TILE), tile)
-        totals = add_up(it, tile)
+        totals = add_up(it, tile, lambda: each(n_lb - 1, to_block))
 
         drain(block_in.at[it, pl.ds(0, n_lb - 1)], s_recv.at[it])
         total = image[half, pl.ds(pl.multiple_of(z * rows, rows), rows), :]
@@ -335,7 +337,7 @@
             total = total + block_in[it, lax.rem(z + j, n_lb)].astype(f32)
         return total, totals
 
-    def add_up(it, tile):
+    def add_up(it, tile, between):
         slot = z * 2 + half
         tiles_a[it, slot] = tile
         tile_out[it] = tile
@@ -351,6 +353,7 @@
 
         each(n_lb - 1, along)
         each(n_lb, across)
+        between()
         drain(tiles_a.at[it, pl.ds(0, 2 * n_lb - 1)], a_recv.at[it])
         tile = tiles_a[it, 0]
         for j in range(1, 2 * n_lb):

time: 172 us -> 129 us (0.75)
  Pallas kernels: 164 us -> 120 us
    pallas_call x1, Pallas kernels: 164 us -> 120 us  [per_device(): pl.pallas_call(functools.partial(kernel, dims), out_shape=(out, out), in_...]
where the time goes in v2:
time: 129 us; the launch traced here: 128 us
  Pallas kernels  120 us (93%)
  local copies, waits for them, and re-layouts  6.31 us (5%)
    pallas_call x1, Pallas kernels, per_device(): pl.pallas_call(functools.partial(kernel, dims), out_shape=(out, out), in_...  120 us

profile of v2, /device:TPU:1, one launch (start us, length us, event | category | flops | bytes accessed | tf_op | source)
XLA Modules:
  0.0 128.4 jit_solution(8144723112005615239)
XLA Ops:
  0.6 0.8 slice_bitcast_fusion.1
  1.4 0.1 broadcast_compare_fusion
  1.5 0.1 iota_compare_fusion
  1.6 0.1 broadcast_and_fusion
  1.6 0.8 fusion
  2.4 0.1 copy.12
  2.5 0.1 select_reduce_fusion
  2.6 0.7 reshape.89.op_ref
  3.3 1.5 %copy.18 = bf16[8,8,4,128]{3,1,2,0:T(8,128)(2,1)} copy(bf16[8,8,4,128]{3,2,1,0:T(4,128)(2,1)} %bitcast.24) | data formatting | bytes 131072
  4.8 120.3 %davidson.1 = (f32[2,64,256]{2,1,0:T(8,128)}, f32[2,64,256]{2,1,0:T(8,128)}) custom-call(bf16[64,512]{1,0:T(8,128)(2,1)} %bitcast.21, bf16[128,8,128]{2,1,0:T(8,128)(2,1)} %right_ref.1, f32[512]{0:T(512)} %reshape.89.op_ref, bf16[4,512,1024]{2,1,0:T(8,128)(2,1)} %bitcast.18), custom_call_target="tpu_custom_call" | custom-call | tf_op jit(solution)/shard_map/davidson/pallas_call | solution.py:470
  125.1 1.0 reshape.91
  126.1 0.7 copy.13
  126.8 1.0 reshape.93
  127.7 0.7 copy.14
  (1 shorter events, 0.0 us)

commit v3 on v2

--- a/solution.py
+++ b/solution.py
@@ -87,7 +87,8 @@
     dims,
     guess_ref,
     right_ref,
-    op_ref,
+    blocks_ref,
+    pairs_ref,
     left_hbm,
     vector_ref,
     residual_ref,
@@ -95,6 +96,7 @@
     mixing,
     right_rows,
     right_by_level,
+    right_diag,
     gathered,
     column,
     inner,
@@ -111,6 +113,8 @@
     tiles_a,
     tile_mid,
     tiles_b,
+    final_out,
+    final_in,
     left_sem,
     x_send,
     x_recv,
@@ -118,6 +122,8 @@
     f_recv,
     z_send,
     z_recv,
+    c_send,
+    c_recv,
     p_send,
     p_recv,
     s_send,
@@ -129,7 +135,7 @@
     d_sems,
     o_sems,
 ):
-    n_lb, n_rb, line, rows, states, window, levels, local_levels = dims
+    n_lb, n_rb, line, rows, states, window, levels, local_levels, count = dims
     lines = n_rb // line
     chunk = line * rows
     half_width = states * window // 2
@@ -181,7 +187,7 @@
 
     def hand_out(it, part):
         own(it)[...] = part
-        column[it, z] = part
+        column[it, half, z] = part
 
     def start_hand_out(it):
         def to_plane(j):
@@ -195,7 +201,7 @@
             remote(own(it), own(it), x_send.at[it], x_recv.at[it, my_line], {"rb": peer}).start()
 
         def to_column(j):
-            remote(column.at[it, z], column.at[it, z], z_send.at[it], z_recv.at[it], {"lb": lax.rem(z + 1 + j, n_lb)}).start()
+            remote(column.at[it, half, z], column.at[it, half, z], z_send.at[it], z_recv.at[it], {"lb": lax.rem(z + 1 + j, n_lb)}).start()
 
         each(n_rb - 1, to_plane)
         each(n_lb - 1, to_column)
@@ -213,16 +219,18 @@
     for v in range(levels):
         right_by_level[v] = right_rows[pl.ds(v, window, stride=levels), :]
 
-    def op_at(w, v, t, s):
-        return op_ref[((w * levels + v) * states + t) * states + s]
+    def factor(n, w, t, s):
+        named = jnp.where(pairs_ref[0, n] == half * local_levels + w, 0.5, 0.0)
+        return named * (blocks_ref[t, s, n] + blocks_ref[s, t, n])
 
     def mix_level(w):
         for t in range(states):
             for s in range(t, states):
-                tile = op_at(w, 0, t, s) * right_by_level[0]
-                for v in range(1, levels):
-                    tile = tile + op_at(w, v, t, s) * right_by_level[v]
-                tile = tile.astype(bf16)
+
+                def add_block(n, tile):
+                    return tile + factor(n, w, t, s) * right_by_level[pairs_ref[1, n]]
+
+                tile = lax.fori_loop(0, count, add_block, jnp.zeros((window, window), f32), unroll=4).astype(bf16)
                 for a, b in {(t, s), (s, t)}:
                     mixing[w, a // 2, b * window : (b + 1) * window, (a % 2) * window : (a % 2 + 1) * window] = tile
 
@@ -230,9 +238,9 @@
 
     row_at = lax.broadcasted_iota(jnp.int32, (window, window), 0)
     col_at = lax.broadcasted_iota(jnp.int32, (window, window), 1)
-    right_diag = [
-        jnp.sum(jnp.where(row_at == col_at, right_by_level[v], 0.0), axis=0, keepdims=True) for v in range(levels)
-    ]
+    for v in range(levels):
+        on_diagonal = jnp.where(row_at == col_at, right_by_level[v], 0.0)
+        right_diag[v] = jnp.broadcast_to(jnp.sum(on_diagonal, axis=0, keepdims=True), TILE)
     each(local_levels * lines, lambda i: left_copy(i).wait())
     q_own = my_line
     inside = lax.rem(me, line) * rows
@@ -244,10 +252,10 @@
         entries = left[q_own, pl.ds(pl.multiple_of(z * rows, rows), rows), w * chunk : (w + 1) * chunk].astype(f32)
         left_diag = jnp.sum(jnp.where(picked, entries, 0.0), axis=1, keepdims=True)
         for s in range(states):
-            along = op_at(w, 0, s, s) * right_diag[0]
-            for v in range(1, levels):
-                along = along + op_at(w, v, s, s) * right_diag[v]
-            parts[s] = parts[s] + left_diag * along
+            along = lax.fori_loop(
+                0, count, lambda n, a, s=s, w=w: a + factor(n, w, s, s) * right_diag[pairs_ref[1, n]], jnp.zeros(TILE, f32)
+            )
+            parts[s] = parts[s] + left_diag * along[0:1]
     for s in range(states):
         diag_parts[s // 2, :, (s % 2) * window : (s % 2 + 1) * window] = parts[s]
     diag_copy = remote(diag_parts.at[other], diag_in, d_sems.at[0], d_sems.at[1], {"wa": other})
@@ -257,11 +265,11 @@
         piece = jnp.broadcast_to(number[0:1, :], (rows, TILE[1]))
         return jnp.concatenate([piece] * (half_width // TILE[1]), axis=1)
 
-    def lane_sums(value):
-        total = jnp.sum(value, axis=0, keepdims=True)
-        out = total[:, : TILE[1]]
+    def fold(value):
+        groups = jnp.sum(value.reshape(rows // TILE[0], TILE[0], half_width), axis=0)
+        out = groups[:, : TILE[1]]
         for i in range(1, half_width // TILE[1]):
-            out = out + total[:, i * TILE[1] : (i + 1) * TILE[1]]
+            out = out + groups[:, i * TILE[1] : (i + 1) * TILE[1]]
         return out
 
     def chunk_rows(q):
@@ -275,6 +283,10 @@
     def forward(it, q):
         region = gathered.at[it, half, chunk_rows(q)]
         return remote(region, region, f_send.at[it, q], f_recv.at[it, q], {"wa": other})
+
+    def forward_column(it):
+        region = column.at[it, half]
+        return remote(region, region, c_send.at[it], c_recv.at[it], {"wa": other})
 
     def multiply(it, q):
         x = jnp.concatenate([gathered[it, 0, chunk_rows(q), :], gathered[it, 1, chunk_rows(q), :]], axis=1)
@@ -299,6 +311,11 @@
                 drain(gathered.at[it, half, chunk_rows(q)], x_recv.at[it, q])
                 forward(it, q).start()
 
+            @pl.when(i == lines - 1)
+            def _():
+                drain(column.at[it, half, pl.ds(0, n_lb - 1)], z_recv.at[it])
+                forward_column(it).start()
+
             q = line_at(i)
             drain(gathered.at[it, other, chunk_rows(q)], f_recv.at[it, q])
             multiply(it, q)
@@ -308,28 +325,32 @@
         pair_out[it] = image[other].astype(bf16)
         pair = remote(pair_out.at[it], pair_in.at[it], p_send.at[it], p_recv.at[it], {"wa": other})
         pair.start()
-        drain(column.at[it, pl.ds(0, n_lb - 1)], z_recv.at[it])
-        sums = [lane_sums(member * member)]
-        sums += [lane_sums(basis[j] * member) for j in range(it)]
-        sums += [lane_sums(images[j] * member) for j in range(it)]
-        pair.wait_recv()
-        product = jnp.zeros((1, TILE[1]), f32)
-        mine = None
-        for b in range(n_lb):
-            summed = image[half, b * rows : (b + 1) * rows, :] + pair_in[it, b * rows : (b + 1) * rows, :].astype(f32)
-            image[half, b * rows : (b + 1) * rows, :] = summed
-            block_out[it, b] = summed.astype(bf16)
-            product = product + lane_sums(summed * column[it, b].astype(f32))
+        sums = [fold(member * member)]
+        sums += [fold(basis[j] * member) for j in range(it)]
+        sums += [fold(images[j] * member) for j in range(it)]
+        drain(column.at[it, other], c_recv.at[it])
+        product = jnp.zeros(TILE, f32)
+        for h in range(2):
+            for b in range(n_lb):
+                product = product + fold(image[h, b * rows : (b + 1) * rows, :] * column[it, h, b].astype(f32))
+        row = lax.broadcasted_iota(jnp.int32, TILE, 0)
+        tile = jnp.zeros(TILE, f32)
+        for i, value in enumerate([product] + sums):
+            value = jnp.sum(value, axis=0, keepdims=True)
+            tile = jnp.where(row == i, jnp.broadcast_to(value, TILE), tile)
 
         def to_block(j):
             b = lax.rem(z + 1 + j, n_lb)
             remote(block_out.at[it, b], block_in.at[it, z], s_send.at[it], s_recv.at[it], {"lb": b}).start()
 
-        row = lax.broadcasted_iota(jnp.int32, TILE, 0)
-        tile = jnp.zeros(TILE, f32)
-        for i, value in enumerate([product] + sums):
-            tile = jnp.where(row == i, jnp.broadcast_to(value, TILE), tile)
-        totals = add_up(it, tile, lambda: each(n_lb - 1, to_block))
+        def exchange_blocks():
+            pair.wait_recv()
+            summed = image[half] + pair_in[it].astype(f32)
+            image[half] = summed
+            block_out[it] = summed.astype(bf16).reshape(n_lb, rows, half_width)
+            each(n_lb - 1, to_block)
+
+        totals = add_up(it, tile, exchange_blocks)
 
         drain(block_in.at[it, pl.ds(0, n_lb - 1)], s_recv.at[it])
         total = image[half, pl.ds(pl.multiple_of(z * rows, rows), rows), :]
@@ -339,33 +360,44 @@
 
     def add_up(it, tile, between):
         slot = z * 2 + half
-        tiles_a[it, slot] = tile
         tile_out[it] = tile
 
-        def along(j):
-            remote(tile_out.at[it], tiles_a.at[it, slot], a_send.at[it], a_recv.at[it], {"lb": lax.rem(z + 1 + j, n_lb)}).start()
-
-        def across(j):
-            remote(
-                tile_out.at[it], tiles_a.at[it, slot], a_send.at[it], a_recv.at[it],
-                {"lb": lax.rem(z + j, n_lb), "wa": other},
-            ).start()
-
-        each(n_lb - 1, along)
-        each(n_lb, across)
+        def to_column(j):
+            peer = {"lb": lax.rem(z + 1 + j, n_lb), "wa": 1}
+            remote(tile_out.at[it], tiles_a.at[it, slot], a_send.at[it], a_recv.at[it], peer).start()
+
+        each(n_lb - 1, to_column)
+
+        @pl.when(half == 0)
+        def _():
+            remote(tile_out.at[it], tiles_a.at[it, slot], a_send.at[it], a_recv.at[it], {"wa": 1}).start()
+
+        @pl.when(half == 1)
+        def _():
+            tiles_a[it, slot] = tile
+
         between()
-        drain(tiles_a.at[it, pl.ds(0, 2 * n_lb - 1)], a_recv.at[it])
-        tile = tiles_a[it, 0]
-        for j in range(1, 2 * n_lb):
-            tile = tile + tiles_a[it, j]
-        tiles_b[it, me] = tile
-        tile_mid[it] = tile
-
-        def plane(j):
-            remote(tile_mid.at[it], tiles_b.at[it, me], b_send.at[it], b_recv.at[it], {"rb": lax.rem(me + 1 + j, n_rb)}).start()
-
-        each(n_rb - 1, plane)
-        drain(tiles_b.at[it, pl.ds(0, n_rb - 1)], b_recv.at[it])
+
+        @pl.when(half == 1)
+        def _():
+            drain(tiles_a.at[it, pl.ds(0, 2 * n_lb - 1)], a_recv.at[it])
+            summed = tiles_a[it, 0]
+            for j in range(1, 2 * n_lb):
+                summed = summed + tiles_a[it, j]
+            tile_mid[it] = summed
+            tiles_b[it, me] = summed
+
+            def to_plane(j):
+                peer = {"rb": lax.rem(me + lax.div(j + 1, 2), n_rb), "wa": lax.rem(j, 2)}
+                remote(tile_mid.at[it], tiles_b.at[it, me], b_send.at[it], b_recv.at[it], peer).start()
+
+            each(2 * n_rb - 1, to_plane)
+            drain(tiles_b.at[it, pl.ds(0, n_rb - 1)], b_recv.at[it])
+
+        @pl.when(half == 0)
+        def _():
+            drain(tiles_b.at[it], b_recv.at[it])
+
         tile = tiles_b[it, 0]
         for j in range(1, n_rb):
             tile = tile + tiles_b[it, j]
@@ -417,36 +449,49 @@
             hand_out(it + 1, current.astype(bf16))
             start_hand_out(it + 1)
 
-    vector_ref[half] = ritz
-    residual_ref[half] = residual
-    copies = [
-        remote(ref.at[half], ref.at[half], o_sems.at[2 * i], o_sems.at[2 * i + 1], {"wa": other})
-        for i, ref in enumerate((vector_ref, residual_ref))
-    ]
-    for copy in copies:
-        copy.start()
+    outputs = (vector_ref, residual_ref)
+    for i, value in enumerate((ritz, residual)):
+        final_out[i] = value
+    last_copy = remote(final_out, final_in, o_sems.at[0], o_sems.at[1], {"wa": other})
+    last_copy.start()
+
+    def put(i, side, value):
+        for k in range(states // 2):
+            outputs[i][pl.ds(side * (states // 2) + k, rows, stride=states), :] = value[:, k * window : (k + 1) * window]
+
+    for side in range(2):
+
+        @pl.when(half == side)
+        def _():
+            for i, value in enumerate((ritz, residual)):
+                put(i, side, value)
 
     def finish(it):
         drain(gathered.at[it, 0, pl.ds(0, (n_rb - 1) * rows)], x_send.at[it])
-        drain(column.at[it, pl.ds(0, n_lb - 1)], z_send.at[it])
+        drain(column.at[it, half, pl.ds(0, n_lb - 1)], z_send.at[it])
+        forward_column(it).wait_send()
         each(lines, lambda q: forward(it, q).wait_send())
         drain(pair_out.at[it], p_send.at[it])
         drain(block_out.at[it, pl.ds(0, n_lb - 1)], s_send.at[it])
-        drain(tiles_a.at[it, pl.ds(0, 2 * n_lb - 1)], a_send.at[it])
-        drain(tiles_b.at[it, pl.ds(0, n_rb - 1)], b_send.at[it])
+        drain(tiles_a.at[it, pl.ds(0, n_lb - 1)], a_send.at[it])
+
+        @pl.when(half == 0)
+        def _():
+            drain(tiles_a.at[it, 0], a_send.at[it])
+
+        @pl.when(half == 1)
+        def _():
+            drain(tiles_b.at[it], b_send.at[it])
+            drain(tiles_b.at[it, pl.ds(0, n_rb - 1)], b_send.at[it])
 
     each(STEPS, finish)
-    for copy in copies:
-        copy.wait()
-
-
-def dense_operator(operator_blocks, operator_pairs, first_level, local_levels, levels):
-    symmetric = 0.5 * (operator_blocks + jnp.swapaxes(operator_blocks, 1, 2))
-    count = symmetric.shape[0]
-    left_hot = operator_pairs[:, 0][:, None] == first_level + jnp.arange(local_levels, dtype=jnp.int32)[None]
-    right_hot = operator_pairs[:, 1][:, None] == jnp.arange(levels, dtype=jnp.int32)[None]
-    hot = left_hot[:, :, None, None] & right_hot[:, None, :, None]
-    return jnp.sum(jnp.where(hot, symmetric.reshape(count, 1, 1, -1), 0.0), axis=0).reshape(-1)
+    last_copy.wait()
+    for side in range(2):
+
+        @pl.when(half == 1 - side)
+        def _():
+            for i in range(2):
+                put(i, side, final_in[i])
 
 
 def per_device(initial_guess, left_environment, right_environment, operator_blocks, operator_pairs):
@@ -459,26 +504,25 @@
     lines, chunk = n_rb // line, line * rows
     width, half_width = states * window, states * window // 2
     block_rows = n_lb * rows
-    operator = dense_operator(
-        operator_blocks, operator_pairs, lax.axis_index("wa") * local_levels, local_levels, levels
-    )
-    dims = (n_lb, n_rb, line, rows, states, window, levels, local_levels)
+    dims = (n_lb, n_rb, line, rows, states, window, levels, local_levels, operator_pairs.shape[0])
     f32, bf16 = jnp.float32, jnp.bfloat16
     dma = pltpu.SemaphoreType.DMA
     vmem = pl.BlockSpec(memory_space=pltpu.VMEM)
-    out = jax.ShapeDtypeStruct((2, rows, half_width), f32)
+    smem = pl.BlockSpec(memory_space=pltpu.SMEM)
+    out = jax.ShapeDtypeStruct((rows * states, window), f32)
     outs = pl.pallas_call(
         functools.partial(kernel, dims),
         out_shape=(out, out),
-        in_specs=[vmem, vmem, pl.BlockSpec(memory_space=pltpu.SMEM), pl.BlockSpec(memory_space=pl.ANY)],
+        in_specs=[vmem, vmem, smem, smem, pl.BlockSpec(memory_space=pl.ANY)],
         out_specs=(vmem, vmem),
         scratch_shapes=[
             pltpu.VMEM((lines, block_rows, local_levels * chunk), bf16),
             pltpu.VMEM((local_levels, 2, width, half_width), bf16),
             pltpu.VMEM((window * levels, window), f32),
             pltpu.VMEM((levels, window, window), f32),
+            pltpu.VMEM((levels, *TILE), f32),
             pltpu.VMEM((STEPS, 2, contracted, half_width), bf16),
-            pltpu.VMEM((STEPS, n_lb, rows, half_width), bf16),
+            pltpu.VMEM((STEPS, 2, n_lb, rows, half_width), bf16),
             pltpu.VMEM((2, local_levels * chunk, half_width), bf16),
             pltpu.VMEM((2, block_rows, half_width), f32),
             pltpu.VMEM((STEPS, block_rows, half_width), bf16),
@@ -493,6 +537,8 @@
             pltpu.VMEM((STEPS, 2 * n_lb, *TILE), f32),
             pltpu.VMEM((STEPS, *TILE), f32),
             pltpu.VMEM((STEPS, n_rb, *TILE), f32),
+            pltpu.VMEM((2, rows, half_width), f32),
+            pltpu.VMEM((2, rows, half_width), f32),
             dma(()),
             dma((STEPS,)),
             dma((STEPS, lines)),
@@ -508,20 +554,21 @@
             dma((STEPS,)),
             dma((STEPS,)),
             dma((STEPS,)),
+            dma((STEPS,)),
+            dma((STEPS,)),
             dma((2,)),
-            dma((4,)),
+            dma((2,)),
         ],
         compiler_params=pltpu.CompilerParams(collective_id=0, has_side_effects=True),
         name="davidson",
     )(
         initial_guess.reshape(rows, width),
         right_environment,
-        operator,
+        operator_blocks.transpose(1, 2, 0),
+        operator_pairs.T,
         left_environment.reshape(local_levels, block_rows, contracted),
     )
-    return tuple(
-        o.reshape(2, rows, states // 2, window).transpose(1, 0, 2, 3).reshape(rows, states, window) for o in outs
-    )
+    return tuple(o.reshape(rows, states, window) for o in outs)
 
 
 def solution(mesh):

time: 129 us -> 120 us (0.930)
  Pallas kernels: 120 us -> 115 us
  local copies, waits for them, and re-layouts: 6.31 us -> 4.61 us
    pallas_call x1, Pallas kernels: 120 us -> 115 us  [per_device(): pl.pallas_call(functools.partial(kernel, dims), out_shape=(out, out), in_...]
    unnamed x1 -> x3, local copies, waits for them, and re-layouts: 1.48 us -> 4.61 us
    reshape x3 -> x0, local copies, waits for them, and re-layouts: 2.6 us -> none  [the longest x2 1.94 us: per_device(): o.reshape(2, rows, states // 2, window).transpose(1, 0, 2, 3)]
    transpose x2 -> x0, local copies, waits for them, and re-layouts: 1.4 us -> none  [per_device(): o.reshape(2, rows, states // 2, window).transpose(1, 0, 2, 3)]
where the time goes in v3:
time: 120 us
  Pallas kernels  115 us (96%)
  local copies, waits for them, and re-layouts  4.61 us (4%)
    pallas_call x1, Pallas kernels, per_device(): pl.pallas_call(functools.partial(kernel, dims), out_shape=(out, out), in_...  115 us
    unnamed x3, local copies, waits for them, and re-layouts  4.61 us

profile of v3, /device:TPU:1, one launch (start us, length us, event | category | flops | bytes accessed | tf_op | source)
XLA Modules:
  0.0 119.9 jit_solution(17792404273045300831)
XLA Ops:
  0.6 1.5 %copy.9 = bf16[8,8,4,128]{3,1,2,0:T(8,128)(2,1)} copy(bf16[8,8,4,128]{3,2,1,0:T(4,128)(2,1)} %bitcast.13) | data formatting | bytes 131072
  2.1 114.7 %davidson.1 = (f32[256,128]{1,0:T(8,128)}, f32[256,128]{1,0:T(8,128)}) custom-call(bf16[64,512]{1,0:T(8,128)(2,1)} %bitcast.10, bf16[128,8,128]{2,1,0:T(8,128)(2,1)} %right_ref.1, f32[4,4,16]{2,1,0:T(4,128)} %bitcast.14, s32[2,16]{1,0:T(2,128)} %bitcast.15, bf16[4,512,1024]{2,1,0:T(8,128)(2,1)} %bitcast.9), custom_call_target="tpu_custom_call" | custom-call | tf_op jit(solution)/shard_map/davidson/pallas_call | solution.py:513
  116.8 1.6 %copy.12 = f32[64,4,128]{2,1,0:T(4,128)} copy(f32[64,4,128]{2,1,0:T(4,128)} %bitcast.12) | data formatting | bytes 262144
  118.3 1.6 %copy.13 = f32[64,4,128]{2,1,0:T(4,128)} copy(f32[64,4,128]{2,1,0:T(4,128)} %bitcast.11) | data formatting | bytes 262144

commit v4 on v3

--- a/solution.py
+++ b/solution.py
@@ -115,6 +115,7 @@
     tiles_b,
     final_out,
     final_in,
+    guess_rows,
     left_sem,
     x_send,
     x_recv,
@@ -145,7 +146,7 @@
     me = lax.axis_index("rb")
     half = lax.axis_index("wa")
     other = 1 - half
-    my_line = lax.div(me, line)
+    my_line, my_place = lax.div(me, line), lax.rem(me, line)
     f32, bf16 = jnp.float32, jnp.bfloat16
 
     def remote(src, dst, send, recv, peer):
@@ -156,12 +157,12 @@
     def drain(region, sem):
         pltpu.make_async_copy(region, region, sem).wait()
 
-    def each(count, body):
+    def each(count, body, unroll=False):
         def step(i, carry):
             body(i)
             return carry
 
-        lax.fori_loop(0, count, step, 0)
+        lax.fori_loop(0, count, step, 0, unroll=unroll)
 
     def left_copy(i):
         w, q = lax.div(i, lines), lax.rem(i, lines)
@@ -182,34 +183,76 @@
     each(n_lb - 1, lambda j: greet({"lb": lax.rem(z + 1 + j, n_lb)}))
     each(n_lb, lambda j: greet({"lb": lax.rem(z + j, n_lb), "wa": other}))
 
-    def own(it):
-        return gathered.at[it, half, pl.ds(pl.multiple_of(me * rows, rows), rows)]
+    def block(it, side, x, y):
+        return gathered.at[it, side, pl.ds(pl.multiple_of((x * line + y) * rows, rows), rows)]
+
+    def send_block(it, x, y, to_x, to_y):
+        region = block(it, half, x, y)
+        peer = {"rb": lax.rem(to_x, lines) * line + lax.rem(to_y, line)}
+        remote(region, region, x_send.at[it], x_recv.at[it, x * line + y], peer).start()
+
+    def forward(it, x, y):
+        region = block(it, half, x, y)
+        remote(region, region, f_send.at[it], f_recv.at[it, x * line + y], {"wa": other}).start()
 
     def hand_out(it, part):
-        own(it)[...] = part
+        block(it, half, my_line, my_place)[...] = part
         column[it, half, z] = part
 
+    def far_first(j, size):
+        step = lax.div(j + 1, 2)
+        return size // 2 + step - 2 * step * lax.rem(j, 2)
+
     def start_hand_out(it):
-        def to_plane(j):
-            j = j + 1
-            away, across = lax.div(j, line), lax.rem(me + j, line)
-            if lines == 4:
-                away = 4 * lax.div(away + 3, 4) - (away + lax.div(away, 2) - 2 * lax.div(away, 3))
-            else:
-                away = lines * lax.div(away + lines - 1, lines) - away
-            peer = lax.rem(my_line + away, lines) * line + across
-            remote(own(it), own(it), x_send.at[it], x_recv.at[it, my_line], {"rb": peer}).start()
+        def to_axes(j):
+            d = far_first(j, line)
+            send_block(it, my_line, my_place, my_line, my_place + d)
+            send_block(it, my_line, my_place, my_line + d, my_place)
 
         def to_column(j):
-            remote(column.at[it, half, z], column.at[it, half, z], z_send.at[it], z_recv.at[it], {"lb": lax.rem(z + 1 + j, n_lb)}).start()
-
-        each(n_rb - 1, to_plane)
+            region = column.at[it, half, z]
+            remote(region, region, z_send.at[it], z_recv.at[it], {"lb": lax.rem(z + 1 + j, n_lb)}).start()
+
+        each(line - 1, to_axes, True)
+        forward(it, my_line, my_place)
         each(n_lb - 1, to_column)
 
-    def own_half(ref):
-        return jnp.where(half == 0, ref[:, :half_width], ref[:, half_width:])
-
-    first = own_half(guess_ref)
+    def pass_on(it):
+        def one(j):
+            d = j + 1 + j - 3 * lax.div(j, 2)
+            on_x = 1 - lax.rem(my_line + my_place + d, 2)
+            x, y = lax.rem(my_line + d * on_x, lines), lax.rem(my_place + d * (1 - on_x), line)
+            drain(block(it, half, x, y), x_recv.at[it, x * line + y])
+
+            def to(k):
+                e = far_first(k, line)
+                send_block(it, x, y, my_line + e * (1 - on_x), my_place + e * on_x)
+
+            each(line - 1, to, True)
+            forward(it, x, y)
+
+        each(line - 1, one)
+
+    def arrive(it, x):
+        for y in range(line):
+            same_x, same_y = x == my_line, my_place == y
+            odd = lax.rem(x + y, 2) == 1
+            done = (same_x & same_y) | (same_y & ~same_x & ~odd) | (same_x & ~same_y & odd)
+
+            @pl.when(jnp.logical_not(done))
+            def _():
+                drain(block(it, half, x, y), x_recv.at[it, x * line + y])
+                forward(it, x, y)
+
+    for r in range(rows):
+        guess_rows[r * states : (r + 1) * states, :] = guess_ref[r].astype(f32)
+    first = jnp.concatenate(
+        [
+            guess_rows[pl.ds(half * (states // 2) + k, rows, stride=states), :].astype(bf16)
+            for k in range(states // 2)
+        ],
+        axis=1,
+    )
     hand_out(0, first)
     current = first.astype(f32)
     pl.semaphore_wait(barrier, (n_rb - 1) + (n_lb - 1) + n_lb)
@@ -262,7 +305,7 @@
     diag_copy.start()
 
     def spread(number):
-        piece = jnp.broadcast_to(number[0:1, :], (rows, TILE[1]))
+        piece = jnp.concatenate([number] * (rows // TILE[0]), axis=0)
         return jnp.concatenate([piece] * (half_width // TILE[1]), axis=1)
 
     def fold(value):
@@ -279,10 +322,6 @@
         if lines == 4:
             i = i + lax.div(i, 2) - 2 * lax.div(i, 3)
         return lax.rem(my_line + i, lines)
-
-    def forward(it, q):
-        region = gathered.at[it, half, chunk_rows(q)]
-        return remote(region, region, f_send.at[it, q], f_recv.at[it, q], {"wa": other})
 
     def forward_column(it):
         region = column.at[it, half]
@@ -299,48 +338,55 @@
         for h in range(2):
             image[h] += jnp.dot(left[q], inner[h], preferred_element_type=f32)
 
+    def row_sums(first_row, values):
+        row = lax.broadcasted_iota(jnp.int32, TILE, 0)
+        tile = jnp.zeros(TILE, f32)
+        for i, value in enumerate(values):
+            value = jnp.sum(value, axis=0, keepdims=True)
+            tile = jnp.where(row == first_row + i, jnp.broadcast_to(value, TILE), tile)
+        return tile
+
     def apply(it, member):
+        pass_on(it)
         image[...] = jnp.zeros_like(image)
-        drain(gathered.at[it, half, pl.ds(0, chunk - rows)], x_recv.at[it, my_line])
-        forward(it, my_line).start()
+        sums = [fold(member * member)]
+        sums += [fold(basis[j] * member) for j in range(it)]
+        sums += [fold(images[j] * member) for j in range(it)]
+        tile_out[it] = row_sums(1, sums)
+        arrive(it, my_line)
+        pair = remote(pair_out.at[it], pair_in.at[it], p_send.at[it], p_recv.at[it], {"wa": other})
 
         def one_line(i):
-            @pl.when(i < lines - 1)
-            def _():
-                q = line_at(i + 1)
-                drain(gathered.at[it, half, chunk_rows(q)], x_recv.at[it, q])
-                forward(it, q).start()
-
             @pl.when(i == lines - 1)
             def _():
                 drain(column.at[it, half, pl.ds(0, n_lb - 1)], z_recv.at[it])
                 forward_column(it).start()
 
             q = line_at(i)
-            drain(gathered.at[it, other, chunk_rows(q)], f_recv.at[it, q])
+            for y in range(line):
+                drain(block(it, other, q, y), f_recv.at[it, q * line + y])
             multiply(it, q)
 
+            @pl.when(i == 0)
+            def _():
+                arrive(it, line_at(1))
+
+            @pl.when(i < lines - 2)
+            def _():
+                arrive(it, line_at(i + 2))
+
         each(lines, one_line)
-
         pair_out[it] = image[other].astype(bf16)
-        pair = remote(pair_out.at[it], pair_in.at[it], p_send.at[it], p_recv.at[it], {"wa": other})
         pair.start()
-        sums = [fold(member * member)]
-        sums += [fold(basis[j] * member) for j in range(it)]
-        sums += [fold(images[j] * member) for j in range(it)]
         drain(column.at[it, other], c_recv.at[it])
         product = jnp.zeros(TILE, f32)
         for h in range(2):
             for b in range(n_lb):
                 product = product + fold(image[h, b * rows : (b + 1) * rows, :] * column[it, h, b].astype(f32))
-        row = lax.broadcasted_iota(jnp.int32, TILE, 0)
-        tile = jnp.zeros(TILE, f32)
-        for i, value in enumerate([product] + sums):
-            value = jnp.sum(value, axis=0, keepdims=True)
-            tile = jnp.where(row == i, jnp.broadcast_to(value, TILE), tile)
+        tile = tile_out[it] + row_sums(0, [product])
 
         def to_block(j):
-            b = lax.rem(z + 1 + j, n_lb)
+            b = lax.rem(z + far_first(j, n_lb), n_lb)
             remote(block_out.at[it, b], block_in.at[it, z], s_send.at[it], s_recv.at[it], {"lb": b}).start()
 
         def exchange_blocks():
@@ -348,15 +394,16 @@
             summed = image[half] + pair_in[it].astype(f32)
             image[half] = summed
             block_out[it] = summed.astype(bf16).reshape(n_lb, rows, half_width)
-            each(n_lb - 1, to_block)
-
-        totals = add_up(it, tile, exchange_blocks)
-
-        drain(block_in.at[it, pl.ds(0, n_lb - 1)], s_recv.at[it])
-        total = image[half, pl.ds(pl.multiple_of(z * rows, rows), rows), :]
-        for j in range(1, n_lb):
-            total = total + block_in[it, lax.rem(z + j, n_lb)].astype(f32)
-        return total, totals
+            each(n_lb - 1, to_block, True)
+
+        def collect():
+            drain(block_in.at[it, pl.ds(0, n_lb - 1)], s_recv.at[it])
+            total = image[half, pl.ds(pl.multiple_of(z * rows, rows), rows), :]
+            for j in range(1, n_lb):
+                total = total + block_in[it, lax.rem(z + j, n_lb)].astype(f32)
+            return total
+
+        return add_up(it, tile, exchange_blocks), collect
 
     def add_up(it, tile, between):
         slot = z * 2 + half
@@ -366,7 +413,7 @@
             peer = {"lb": lax.rem(z + 1 + j, n_lb), "wa": 1}
             remote(tile_out.at[it], tiles_a.at[it, slot], a_send.at[it], a_recv.at[it], peer).start()
 
-        each(n_lb - 1, to_column)
+        each(n_lb - 1, to_column, True)
 
         @pl.when(half == 0)
         def _():
@@ -391,7 +438,7 @@
                 peer = {"rb": lax.rem(me + lax.div(j + 1, 2), n_rb), "wa": lax.rem(j, 2)}
                 remote(tile_mid.at[it], tiles_b.at[it, me], b_send.at[it], b_recv.at[it], peer).start()
 
-            each(2 * n_rb - 1, to_plane)
+            each(2 * n_rb - 1, to_plane, True)
             drain(tiles_b.at[it, pl.ds(0, n_rb - 1)], b_recv.at[it])
 
         @pl.when(half == 0)
@@ -407,7 +454,7 @@
     entries = [[None] * STEPS for _ in range(STEPS)]
     diagonal = None
     for it in range(STEPS):
-        applied, totals = apply(it, current)
+        totals, collect = apply(it, current)
         energy, square = totals[0], totals[1]
         overlaps, crossed = totals[2 : 2 + it], totals[2 + it :]
         norm = square
@@ -423,7 +470,7 @@
         entries[it][it] = inverse * inverse * energy
         theta, weights = lowest(entries, it + 1)
 
-        vector, applied_now = current, applied
+        vector, applied_now = current, collect()
         for j in range(it):
             a = spread(overlaps[j])
             vector = vector - a * basis[j]
@@ -470,7 +517,7 @@
         drain(gathered.at[it, 0, pl.ds(0, (n_rb - 1) * rows)], x_send.at[it])
         drain(column.at[it, half, pl.ds(0, n_lb - 1)], z_send.at[it])
         forward_column(it).wait_send()
-        each(lines, lambda q: forward(it, q).wait_send())
+        drain(gathered.at[it, half], f_send.at[it])
         drain(pair_out.at[it], p_send.at[it])
         drain(block_out.at[it, pl.ds(0, n_lb - 1)], s_send.at[it])
         drain(tiles_a.at[it, pl.ds(0, n_lb - 1)], a_send.at[it])
@@ -513,7 +560,7 @@
     outs = pl.pallas_call(
         functools.partial(kernel, dims),
         out_shape=(out, out),
-        in_specs=[vmem, vmem, smem, smem, pl.BlockSpec(memory_space=pl.ANY)],
+        in_specs=[vmem, vmem, smem, smem, pl.BlockSpec(memory_space=pltpu.HBM)],
         out_specs=(vmem, vmem),
         scratch_shapes=[
             pltpu.VMEM((lines, block_rows, local_levels * chunk), bf16),
@@ -539,11 +586,12 @@
             pltpu.VMEM((STEPS, n_rb, *TILE), f32),
             pltpu.VMEM((2, rows, half_width), f32),
             pltpu.VMEM((2, rows, half_width), f32),
+            pltpu.VMEM((rows * states, window), f32),
             dma(()),
             dma((STEPS,)),
-            dma((STEPS, lines)),
-            dma((STEPS, lines)),
-            dma((STEPS, lines)),
+            dma((STEPS, n_rb)),
+            dma((STEPS,)),
+            dma((STEPS, n_rb)),
             dma((STEPS,)),
             dma((STEPS,)),
             dma((STEPS,)),
@@ -562,7 +610,7 @@
         compiler_params=pltpu.CompilerParams(collective_id=0, has_side_effects=True),
         name="davidson",
     )(
-        initial_guess.reshape(rows, width),
+        initial_guess,
         right_environment,
         operator_blocks.transpose(1, 2, 0),
         operator_pairs.T,

time: 120 us -> 116 us (0.967)
  Pallas kernels: 115 us -> 112 us
  local copies, waits for them, and re-layouts: 4.61 us -> 3.14 us
    pallas_call x1, Pallas kernels: 115 us -> 112 us  [per_device(): pl.pallas_call(functools.partial(kernel, dims), out_shape=(out, out), in_...]
    unnamed x3 -> x2, local copies, waits for them, and re-layouts: 4.61 us -> 3.14 us
where the time goes in v4:
time: 116 us
  Pallas kernels  112 us (97%)
  local copies, waits for them, and re-layouts  3.14 us (3%)
    pallas_call x1, Pallas kernels, per_device(): pl.pallas_call(functools.partial(kernel, dims), out_shape=(out, out), in_...  112 us
    unnamed x2, local copies, waits for them, and re-layouts  3.14 us

profile of v4, /device:TPU:1, one launch (start us, length us, event | category | flops | bytes accessed | tf_op | source)
XLA Modules:
  0.0 115.6 jit_solution(9850279721676652633)
XLA Ops:
  0.6 111.8 %davidson.1 = (f32[256,128]{1,0:T(8,128)}, f32[256,128]{1,0:T(8,128)}) custom-call(bf16[64,4,128]{2,1,0:T(4,128)(2,1)} %guess_ref.1, bf16[128,8,128]{2,1,0:T(8,128)(2,1)} %right_ref.1, f32[4,4,16]{2,1,0:T(4,128)} %bitcast.8, s32[2,16]{1,0:T(2,128)} %bitcast.9, bf16[4,512,1024]{2,1,0:T(8,128)(2,1)} %bitcast.5), custom_call_target="tpu_custom_call" | custom-call | tf_op jit(solution)/shard_map/davidson/pallas_call | solution.py:560
  112.4 1.6 %copy.9 = f32[64,4,128]{2,1,0:T(4,128)} copy(f32[64,4,128]{2,1,0:T(4,128)} %bitcast.7) | data formatting | bytes 262144
  114.0 1.6 %copy.10 = f32[64,4,128]{2,1,0:T(4,128)} copy(f32[64,4,128]{2,1,0:T(4,128)} %bitcast.6) | data formatting | bytes 262144

commit v5 on v4

--- a/solution.py
+++ b/solution.py
@@ -277,7 +277,10 @@
                 for a, b in {(t, s), (s, t)}:
                     mixing[w, a // 2, b * window : (b + 1) * window, (a % 2) * window : (a % 2 + 1) * window] = tile
 
-    each(local_levels, mix_level)
+    early = local_levels // 2
+    each(early, mix_level)
+    pass_on(0)
+    each(local_levels - early, lambda w: mix_level(w + early))
 
     row_at = lax.broadcasted_iota(jnp.int32, (window, window), 0)
     col_at = lax.broadcasted_iota(jnp.int32, (window, window), 1)
@@ -347,7 +350,8 @@
         return tile
 
     def apply(it, member):
-        pass_on(it)
+        if it > 0:
+            pass_on(it)
         image[...] = jnp.zeros_like(image)
         sums = [fold(member * member)]
         sums += [fold(basis[j] * member) for j in range(it)]

time: 116 us -> 115 us (level)
  no operation moved by 1% of the time
where the time goes in v5:
time: 115 us
  Pallas kernels  111 us (97%)
  local copies, waits for them, and re-layouts  3.14 us (3%)
    pallas_call x1, Pallas kernels, per_device(): pl.pallas_call(functools.partial(kernel, dims), out_shape=(out, out), in_...  111 us
    unnamed x2, local copies, waits for them, and re-layouts  3.14 us

profile of v5, /device:TPU:1, one launch (start us, length us, event | category | flops | bytes accessed | tf_op | source)
XLA Modules:
  0.0 114.8 jit_solution(122856834166343869)
XLA Ops:
  0.6 111.0 %davidson.1 = (f32[256,128]{1,0:T(8,128)}, f32[256,128]{1,0:T(8,128)}) custom-call(bf16[64,4,128]{2,1,0:T(4,128)(2,1)} %guess_ref.1, bf16[128,8,128]{2,1,0:T(8,128)(2,1)} %right_ref.1, f32[4,4,16]{2,1,0:T(4,128)} %bitcast.8, s32[2,16]{1,0:T(2,128)} %bitcast.9, bf16[4,512,1024]{2,1,0:T(8,128)(2,1)} %bitcast.5), custom_call_target="tpu_custom_call" | custom-call | tf_op jit(solution)/shard_map/davidson/pallas_call | solution.py:564
  111.6 1.6 %copy.9 = f32[64,4,128]{2,1,0:T(4,128)} copy(f32[64,4,128]{2,1,0:T(4,128)} %bitcast.7) | data formatting | bytes 262144
  113.2 1.6 %copy.10 = f32[64,4,128]{2,1,0:T(4,128)} copy(f32[64,4,128]{2,1,0:T(4,128)} %bitcast.6) | data formatting | bytes 262144

commit v6 on v5

--- a/solution.py
+++ b/solution.py
@@ -277,7 +277,7 @@
                 for a, b in {(t, s), (s, t)}:
                     mixing[w, a // 2, b * window : (b + 1) * window, (a % 2) * window : (a % 2 + 1) * window] = tile
 
-    early = local_levels // 2
+    early = 1
     each(early, mix_level)
     pass_on(0)
     each(local_levels - early, lambda w: mix_level(w + early))
@@ -481,8 +481,6 @@
             applied_now = applied_now - a * images[j]
         grow = spread(inverse)
         vector, applied_now = vector * grow, applied_now * grow
-        basis[it] = vector
-        images[it] = applied_now
         last = spread(weights[it])
         ritz, residual = last * vector, last * applied_now
         for j in range(it):
@@ -499,6 +497,8 @@
             current = residual / (jnp.abs(diag_parts[half] - shift) + 1.0)
             hand_out(it + 1, current.astype(bf16))
             start_hand_out(it + 1)
+            basis[it] = vector
+            images[it] = applied_now
 
     outputs = (vector_ref, residual_ref)
     for i, value in enumerate((ritz, residual)):

time: 115 us -> 116 us (level)
  Pallas kernels: 111 us -> 113 us
    pallas_call x1, Pallas kernels: 111 us -> 113 us  [per_device(): pl.pallas_call(functools.partial(kernel, dims), out_shape=(out, out), in_...]
where the time goes in v6:
time: 116 us
  Pallas kernels  113 us (97%)
  local copies, waits for them, and re-layouts  3.14 us (3%)
    pallas_call x1, Pallas kernels, per_device(): pl.pallas_call(functools.partial(kernel, dims), out_shape=(out, out), in_...  113 us
    unnamed x2, local copies, waits for them, and re-layouts  3.14 us

profile of v6, /device:TPU:1, one launch (start us, length us, event | category | flops | bytes accessed | tf_op | source)
XLA Modules:
  0.0 116.3 jit_solution(8422180681667683534)
XLA Ops:
  0.6 112.6 %davidson.1 = (f32[256,128]{1,0:T(8,128)}, f32[256,128]{1,0:T(8,128)}) custom-call(bf16[64,4,128]{2,1,0:T(4,128)(2,1)} %guess_ref.1, bf16[128,8,128]{2,1,0:T(8,128)(2,1)} %right_ref.1, f32[4,4,16]{2,1,0:T(4,128)} %bitcast.8, s32[2,16]{1,0:T(2,128)} %bitcast.9, bf16[4,512,1024]{2,1,0:T(8,128)(2,1)} %bitcast.5), custom_call_target="tpu_custom_call" | custom-call | tf_op jit(solution)/shard_map/davidson/pallas_call | solution.py:564
  113.2 1.6 %copy.9 = f32[64,4,128]{2,1,0:T(4,128)} copy(f32[64,4,128]{2,1,0:T(4,128)} %bitcast.7) | data formatting | bytes 262144
  114.8 1.6 %copy.10 = f32[64,4,128]{2,1,0:T(4,128)} copy(f32[64,4,128]{2,1,0:T(4,128)} %bitcast.6) | data formatting | bytes 262144
